TPU v7x, 32 devices: a whole 2x2x4 slice. The times are simulated.
32 devices in a mesh: data: 2 (over x), pp: 4 (over z), ep: 4 (over y, core).
Axes of the slice: x: 2, y: 2, z: 4, core: 2. Of those that a mesh axis runs over, the one named last changes fastest.
Arguments:
- expert_out: bfloat16 [8, 64, 320, 2048], P(('data', 'pp'), 'ep'), parts along dimension 0
- expert_ids: int32 [8, 4, 512, 8], P(('data', 'pp'), 'ep'), parts along dimension 0
- slot_ids: int32 [8, 4, 512, 8], P(('data', 'pp'), 'ep'), parts along dimension 0
- gate_vals: float32 [8, 4, 512, 8], P(('data', 'pp'), 'ep'), parts along dimension 0
- residual: bfloat16 [8, 4, 512, 2048], P(('data', 'pp'), 'ep'), parts along dimension 0
- norm_scale: float32 [4, 2048], P('pp')
- w_query: bfloat16 [4, 2048, 16, 128], P('pp')
- w_key: bfloat16 [4, 2048, 16, 128], P('pp')
- w_value: bfloat16 [4, 2048, 16, 128], P('pp')
- w_out: bfloat16 [4, 16, 128, 2048], P('pp')
Outputs:
- output: bfloat16 [8, 4, 512, 2048], P(('data', 'pp'), 'ep'), parts along dimension 0
There are 2 independent parts. A program takes and returns all parts, laid end to end along the dimension named above; an argument that names none is the same for every part.
All inputs are finite; a program needn't handle non-finite values.
Results may differ from a plain program's by a relative error of at most 0.02.
Values are sent between devices in bfloat16 or wider.
A program may use at most 1 GiB of HBM per device.

v0:
```python
import jax
import jax.numpy as jnp
from jax import lax
from jax.sharding import PartitionSpec as P

NORM_EPS = 1e-6


def attn_block(merged, scale_vec, w_query, w_key, w_value, w_out):
    head_dim = w_query.shape[-1]
    seq_len = merged.shape[1]
    resid_f32 = merged.astype(jnp.float32)
    inv_rms = lax.rsqrt(jnp.mean(resid_f32 * resid_f32, axis=-1, keepdims=True) + NORM_EPS)
    normed_in = (resid_f32 * inv_rms * scale_vec).astype(jnp.bfloat16)
    q_heads = jnp.einsum('bld,dhe->blhe', normed_in, w_query, preferred_element_type=jnp.float32).astype(jnp.bfloat16)
    k_heads = jnp.einsum('bld,dhe->blhe', normed_in, w_key, preferred_element_type=jnp.float32).astype(jnp.bfloat16)
    v_heads = jnp.einsum('bld,dhe->blhe', normed_in, w_value, preferred_element_type=jnp.float32).astype(jnp.bfloat16)
    scores = jnp.einsum('bqhe,bkhe->bhqk', q_heads, k_heads, preferred_element_type=jnp.float32) * (head_dim ** -0.5)
    causal = jnp.arange(seq_len)[:, None] >= jnp.arange(seq_len)[None, :]
    scores = jnp.where(causal, scores, -1e30)
    exp_scores = jnp.exp(scores - jnp.max(scores, axis=-1, keepdims=True))
    row_sums = jnp.sum(exp_scores, axis=-1)
    mixed_vals = jnp.einsum('bhqk,bkhe->bqhe', exp_scores.astype(jnp.bfloat16), v_heads, preferred_element_type=jnp.float32)
    attn_out = (mixed_vals / jnp.swapaxes(row_sums, -1, -2)[..., None]).astype(jnp.bfloat16)
    proj_out = jnp.einsum('crif,ife->cre', attn_out, w_out, preferred_element_type=jnp.float32).astype(jnp.bfloat16)
    return (resid_f32 + proj_out.astype(jnp.float32)).astype(jnp.bfloat16)


def solution(mesh):
    ep_size = mesh.shape['ep']
    pp_size = mesh.shape['pp']
    next_stage = [(source, (source + 1) % pp_size) for source in range(pp_size)]
    token_spec = P(('data', 'pp'), 'ep', None, None)
    weight_spec = P('pp', None, None, None)

    def body(expert_out, expert_ids, slot_ids, gate_vals, residual, norm_scale, w_query, w_key, w_value, w_out):
        local_experts, capacity, model_width = expert_out.shape[1:]
        cap_dev = capacity // ep_size
        send_buf = expert_out[0].reshape(local_experts, ep_size, cap_dev, model_width)
        received = lax.all_to_all(send_buf, 'ep', 1, 0, tiled=True).reshape(-1, model_width)
        kept_mask = slot_ids[0] >= 0
        local_slot = slot_ids[0] - lax.axis_index('ep') * cap_dev
        row_ids = jnp.where(kept_mask, expert_ids[0] * cap_dev + local_slot, 0)
        gate_used = jnp.where(kept_mask, gate_vals[0], 0.0)
        picked_rows = jnp.take(received, row_ids, axis=0)
        merged = (residual[0].astype(jnp.float32) + jnp.sum(picked_rows * gate_used[..., None], axis=-2)).astype(jnp.bfloat16)
        arrived = lax.ppermute(merged, 'pp', next_stage)
        result = attn_block(arrived, norm_scale[0], w_query[0], w_key[0], w_value[0], w_out[0])
        return result[None]

    return jax.shard_map(body, mesh=mesh, in_specs=(token_spec, token_spec, token_spec, token_spec, token_spec, P('pp', None), weight_spec, weight_spec, weight_spec, weight_spec), out_specs=token_spec, check_vma=False)
```

profile of v0, /device:TPU:0, one launch (start us, length us, event | category | flops | bytes accessed | tf_op | source)
XLA Modules:
  0.0 425.2 jit_solution(3075180755115643601)
XLA Ops:
  0.0 17.6 %copy.17 = bf16[16,4,80,2048]{3,2,0,1:T(8,128)(2,1)} copy(bf16[16,4,80,2048]{3,2,1,0:T(8,128)(2,1)} %bitcast.88) | data formatting | bytes 41943040 | tf_op jit(solution)/shard_map/reshape;squeeze | solution.py:39
  17.6 0.0 copy-start.1
  17.6 0.0 copy-start.2
  17.6 0.0 copy-start.3
  17.6 7.8 %all-to-all-start = ((bf16[16,4,80,2048]{3,2,0,1:T(8,128)(2,1)}), bf16[16,4,80,2048]{3,2,0,1:T(8,128)(2,1)}, u32[]{:S(2)}, u32[]{:S(2)}) async-start(bf16[16,4,80,2048]{3,2,0,1:T(8,128)(2,1)} %copy.17), calls=%async_computation | async-start | bytes 41943040 | tf_op jit(solution)/shard_map/all_to_all | solution.py:40
  25.5 0.0 copy-done.1
  25.5 0.0 copy-done.2
  25.5 0.1 copy.18
  25.6 0.2 reshape.236
  25.8 0.0 copy-done.3
  25.8 0.1 copy.19
  26.0 0.2 copy.16
  26.2 227.6 %all-to-all-done = bf16[16,4,80,2048]{3,2,0,1:T(8,128)(2,1)} async-done(((bf16[16,4,80,2048]{3,2,0,1:T(8,128)(2,1)}), bf16[16,4,80,2048]{3,2,0,1:T(8,128)(2,1)}, u32[]{:S(2)}, u32[]{:S(2)}) %all-to-all-start) | async-done | bytes 20971552 | tf_op jit(solution)/shard_map/all_to_all | solution.py:40
  253.8 41.0 %gather_fusion = bf16[4096,2048]{1,0:T(8,128)(2,1)} fusion(bf16[5120,2048]{1,0:T(8,128)(2,1)} %bitcast.5, s32[4096]{0:T(1024)S(1)} %broadcast_clamp_fusion), kind=kCustom, calls=%fused_computation | custom fusion | bytes 33570816 | tf_op jit(solution)/shard_map/jit(_take)/gather | solution.py:45
  294.8 0.0 copy-start
  294.8 17.7 %multiply_reduce_fusion = f32[512,2048]{1,0:T(8,128)S(1)} fusion(bf16[4096,2048]{1,0:T(8,128)(2,1)} %gather_fusion, f32[512,8]{1,0:T(8,128)S(1)} %copy.19, pred[512,8]{1,0:T(8,128)(4,1)S(1)} %copy.16), kind=kLoop, calls=%fused_computation.1 | loop fusion | flops 32505856 | bytes 20992000 | tf_op jit(solution)/shard_map/reduce_sum | solution.py:46
  312.5 0.0 copy-done
  312.5 0.0 copy-start.4
  312.5 0.7 fusion.22
  313.3 2.7 collective-permute-start
  315.9 0.1 iota_compare_fusion
  316.0 47.8 %collective-permute-done = bf16[1,512,2048]{2,1,0:T(8,128)(2,1)S(1)} collective-permute-done((bf16[1,512,2048]{2,1,0:T(8,128)(2,1)S(1)}, bf16[1,512,2048]{2,1,0:T(8,128)(2,1)S(1)}, u32[]{:S(2)}, u32[]{:S(2)}) %collective-permute-start) | collective-permute-done | bytes 2097184 | tf_op jit(solution)/shard_map/ppermute | solution.py:47
  363.9 0.5 fusion.17
  364.3 0.0 copy-done.4
  364.4 9.3 %fusion.9 = bf16[512,16,128]{2,0,1:T(8,128)(2,1)} fusion(bf16[2048,16,128]{2,1,0:T(8,128)(2,1)} %bitcast.90, bf16[1,512,2048]{2,1,0:T(8,128)(2,1)S(1)} %collective-permute-done, f32[2048]{0:T(1024)S(1)} %bitcast.93, f32[512]{0:T(512)S(1)} %add_rsqrt_fusion), kind=kOutput, calls=%fused_computation.13 | convolution fusion | flops 4299161600 | bytes 12593152 | tf_op jit(solution)/shard_map/bld,dhe->blhe/dot_general | solution.py:15
  373.6 13.2 %fusion = (f32[16,512]{1,0:T(8,128)S(1)}, f32[16,512,512]{1,2,0:T(8,128)}) fusion(pred[512,512]{0,1:T(8,128)(4,1)S(1)} %iota_compare_fusion, bf16[512,16,128]{2,0,1:T(8,128)(2,1)} %fusion.9, bf16[2048,16,128]{2,1,0:T(8,128)(2,1)} %bitcast.91, bf16[1,512,2048]{2,1,0:T(8,128)(2,1)S(1)} %collective-permute-done, f32[2048]{0:T(1024)S(1)} %bitcast.94, ...), kind=kOutput, calls=%fused_computation.5 | convolution fusion | flops 5386526720 | bytes 29665280 | tf_op jit(solution)/shard_map/bqhe,bkhe->bhqk/dot_general | solution.py:18
  386.8 9.2 %fusion.1 = f32[16,512]{1,0:T(8,128)S(1)} fusion(f32[16,512,512]{1,2,0:T(8,128)} %get-tuple-element.6, f32[16,512]{1,0:T(8,128)S(1)} %get-tuple-element.5, pred[512,512]{0,1:T(8,128)(4,1)S(1)} %iota_compare_fusion), kind=kLoop, calls=%fused_computation.6 | loop fusion | flops 16769024 | bytes 17104896 | tf_op jit(solution)/shard_map/reduce_sum | solution.py:22
  396.0 13.0 %fusion.11 = bf16[512,16,128]{0,2,1:T(8,128)(2,1)} fusion(bf16[2048,16,128]{2,1,0:T(8,128)(2,1)} %bitcast.92, bf16[1,512,2048]{2,1,0:T(8,128)(2,1)S(1)} %collective-permute-done, f32[2048]{0:T(1024)S(1)} %bitcast.95, f32[512]{0:T(512)S(1)} %add_rsqrt_fusion), kind=kOutput, calls=%fused_computation.15 | convolution fusion | flops 4299161600 | bytes 12593152 | tf_op jit(solution)/shard_map/bld,dhe->blhe/dot_general | solution.py:17
  409.0 16.2 %fusion.30 = bf16[1,1,512,2048]{3,2,1,0:T(8,128)(2,1)} fusion(bf16[1,16,128,2048]{3,2,1,0:T(8,128)(2,1)} %param.19, bf16[1,512,2048]{2,1,0:T(8,128)(2,1)S(1)} %collective-permute-done, f32[16,512,512]{1,2,0:T(8,128)} %get-tuple-element.6, f32[16,512]{1,0:T(8,128)S(1)} %get-tuple-element.5, pred[512,512]{0,1:T(8,128)(4,1)S(1)} %iota_compare_fusion, ...), kind=kOutput, calls=%fused_computation.34 | convolution fusion | flops 5392826368 | bytes 31784960 | tf_op jit(solution)/shard_map/crif,ife->cre/dot_general | solution.py:25
  (5 shorter events, 0.0 us)
Async XLA Ops:
  17.6 7.9 %copy-start.1 = (s32[1,1,512,8]{2,3,1,0:T(8,128)S(1)}, s32[1,1,512,8]{2,3,1,0:T(8,128)}, u32[]{:S(2)}) copy-start(s32[1,1,512,8]{2,3,1,0:T(8,128)} %param.12) | copy-start | bytes 49156
  17.6 7.9 %copy-start.2 = (s32[1,1,512,8]{2,3,1,0:T(8,128)S(1)}, s32[1,1,512,8]{2,3,1,0:T(8,128)}, u32[]{:S(2)}) copy-start(s32[1,1,512,8]{2,3,1,0:T(8,128)} %param.11) | copy-start | bytes 49156
  17.6 8.2 %copy-start.3 = (f32[1,1,512,8]{2,3,1,0:T(8,128)S(1)}, f32[1,1,512,8]{2,3,1,0:T(8,128)}, u32[]{:S(2)}) copy-start(f32[1,1,512,8]{2,3,1,0:T(8,128)} %param.13) | copy-start | bytes 49156
  17.6 236.2 %all-to-all-start = ((bf16[16,4,80,2048]{3,2,0,1:T(8,128)(2,1)}), bf16[16,4,80,2048]{3,2,0,1:T(8,128)(2,1)}, u32[]{:S(2)}, u32[]{:S(2)}) async-start(bf16[16,4,80,2048]{3,2,0,1:T(8,128)(2,1)} %copy.17), calls=%async_computation | async-start | bytes 41943040 | tf_op jit(solution)/shard_map/all_to_all | solution.py:40
  294.8 17.7 %copy-start = (bf16[1,1,512,2048]{3,2,1,0:T(8,128)(2,1)S(1)}, bf16[1,1,512,2048]{3,2,1,0:T(8,128)(2,1)}, u32[]{:S(2)}) copy-start(bf16[1,1,512,2048]{3,2,1,0:T(8,128)(2,1)} %param.14) | copy-start | bytes 6291460
  312.5 51.8 %copy-start.4 = (f32[1,2048]{1,0:T(1,128)S(1)}, f32[1,2048]{1,0:T(1,128)}, u32[]{:S(2)}) copy-start(f32[1,2048]{1,0:T(1,128)} %param.15) | copy-start | bytes 24580
  313.3 50.6 %collective-permute-start = (bf16[1,512,2048]{2,1,0:T(8,128)(2,1)S(1)}, bf16[1,512,2048]{2,1,0:T(8,128)(2,1)S(1)}, u32[]{:S(2)}, u32[]{:S(2)}) collective-permute-start(bf16[1,512,2048]{2,1,0:T(8,128)(2,1)S(1)} %fusion.22), channel_id=1, source_target_pairs={{0,4},{4,8},{8,12},{12,0},{1,5},{5,9},{9,13},{13,1},{2,6},{6,10},{... | collective-permute-start | bytes 6291464 | tf_op jit(solution)/shard_map/ppermute | solution.py:47
where the time goes:
time: 426 us; the launch traced here: 425 us
  waiting for transfers between devices  275 us (65%)
  local copies, waits for them, and re-layouts  59.2 us (14%)
  matrix products  51.7 us (12%)
  other arithmetic  28.3 us (7%)
  starting transfers between devices  10.5 us (2%)
    all_to_all x1, waiting for transfers between devices, body(): lax.all_to_all(send_buf, 'ep', 1, 0, tiled=True).reshape(-1, model_width)  228 us
    ppermute x1, waiting for transfers between devices, body(): arrived = lax.ppermute(merged, 'pp', next_stage)  47.8 us
    gather x1, local copies, waits for them, and re-layouts, body(): picked_rows = jnp.take(received, row_ids, axis=0)  41 us
    reduce_sum x1, other arithmetic, body(): jnp.sum(picked_rows * gate_used[..., None], axis=-2)  17.7 us
    another operation x1, local copies, waits for them, and re-layouts, body(): expert_out[0].reshape(local_experts, ep_size, cap_dev, model_width)  17.6 us
    dot_general x1, matrix products, attn_block(): jnp.einsum('crif,ife->cre', attn_out, w_out, preferred_element_type=jnp.f...  16.2 us
    dot_general x1, matrix products, attn_block(): jnp.einsum('bqhe,bkhe->bhqk', q_heads, k_heads, preferred_element_type=jn...  13.2 us
    dot_general x1, matrix products, attn_block(): jnp.einsum('bld,dhe->blhe', normed_in, w_value, preferred_element_type=jn...  13 us
  transfers between devices with their start and end apart: 2, of which 2 were waited for; matrix products, arithmetic and copies ran while one was open for 0% of the time, Pallas kernels for 0%

commit v1 on v0

--- a/solution.py
+++ b/solution.py
@@ -1,9 +1,218 @@
+import functools
+
 import jax
 import jax.numpy as jnp
 from jax import lax
+from jax.experimental import pallas as pl
+from jax.experimental.pallas import tpu as pltpu
 from jax.sharding import PartitionSpec as P
 
 NORM_EPS = 1e-6
+MESH = pl.DeviceIdType.MESH
+TOK = 128
+COL = 512
+
+
+def combine_kernel(pp_size, o_hbm, tbl_in, h_hbm, out_hbm, o_buf, tbl, tblt, gmat, ysend, acc, yrecv, dsend, drecv, hz, zrecv,
+                   o_sem, h_sem, t_ssem, t_rsem, d_ssem, d_rsem, credit, y_ssem, y_rsem, z_ssem, z_rsem, out_sem):
+    experts, cap_all, width = o_hbm.shape
+    cap = o_buf.shape[2]
+    slots = experts * cap
+    tokens = h_hbm.shape[0]
+    n_tok, n_col = tokens // TOK, width // COL
+    n_piece = n_tok * n_col
+    me = lax.axis_index('ep')
+    core = lax.rem(me, 2)
+    row = me // 2
+    partner = row * 2 + (1 - core)
+    peer = (1 - row) * 2 + core
+    diag = (1 - row) * 2 + (1 - core)
+    owners = (diag, peer, partner, me)
+    stage = lax.axis_index('pp')
+    nxt = lax.rem(stage + 1, pp_size)
+    prv = lax.rem(stage + pp_size - 1, pp_size)
+
+    def o_copy(r, d):
+        cols = pl.ds(d * COL, COL)
+        return pltpu.make_async_copy(o_hbm.at[:, pl.ds(owners[r] * cap, cap), cols], o_buf.at[r, :, :, cols], o_sem.at[r, d])
+
+    def h_copy(i):
+        c, d = i // n_col, i % n_col
+        return pltpu.make_async_copy(h_hbm.at[pl.ds(c * TOK, TOK), pl.ds(d * COL, COL)], hz.at[i], h_sem.at[i])
+
+    def t_copy(r):
+        return pltpu.make_async_remote_copy(src_ref=tbl_in, dst_ref=tbl.at[r], send_sem=t_ssem.at[r], recv_sem=t_rsem.at[r],
+                                            device_id={'ep': owners[r]}, device_id_type=MESH)
+
+    def d_copy(kind, d):
+        return pltpu.make_async_remote_copy(src_ref=dsend.at[kind, d], dst_ref=drecv.at[kind, d], send_sem=d_ssem.at[kind, d],
+                                            recv_sem=d_rsem.at[kind, d], device_id={'ep': partner}, device_id_type=MESH)
+
+    def y_copy(i):
+        return pltpu.make_async_remote_copy(src_ref=ysend.at[i], dst_ref=yrecv.at[i], send_sem=y_ssem.at[i], recv_sem=y_rsem.at[i],
+                                            device_id={'ep': peer}, device_id_type=MESH)
+
+    def z_copy(i):
+        c, d = i // n_col, i % n_col
+        return pltpu.make_async_remote_copy(src_ref=hz.at[i], dst_ref=zrecv.at[c, :, pl.ds(pl.multiple_of(d * COL, COL), COL)],
+                                            send_sem=z_ssem.at[i], recv_sem=z_rsem.at[i], device_id={'pp': nxt}, device_id_type=MESH)
+
+    for d in range(n_col):
+        for r in range(4):
+            o_copy(r, d).start()
+    for i in range(n_piece):
+        h_copy(i).start()
+
+    barrier = pltpu.get_barrier_semaphore()
+    for dev in (partner, peer, diag):
+        pl.semaphore_signal(barrier, inc=1, device_id={'ep': dev}, device_id_type=MESH)
+    for dev in (nxt, prv):
+        pl.semaphore_signal(barrier, inc=1, device_id={'pp': dev}, device_id_type=MESH)
+    pl.semaphore_wait(barrier, 5)
+
+    for r in range(3):
+        t_copy(r).start()
+    tblt[3] = jnp.transpose(tbl_in[...])
+    for r in range(3):
+        t_copy(r).wait_recv()
+        tblt[r] = jnp.transpose(tbl[r])
+
+    base = (me * slots).astype(jnp.float32)
+
+    def build(c):
+        def rows(k, _):
+            r, q = k // (TOK // 16), k % (TOK // 16)
+            t = tblt[r, pl.ds(pl.multiple_of(c * TOK + q * 16, 16), 16), :]
+            lane = lax.broadcasted_iota(jnp.int32, (16, slots), 1).astype(jnp.float32) + base
+            g = jnp.zeros((16, slots), jnp.float32)
+            for j in range(8):
+                g = jnp.where(lane == t[:, j:j + 1], t[:, 8 + j:9 + j], g)
+            g1 = g.astype(jnp.bfloat16)
+            rest = g - g1.astype(jnp.float32)
+            g2 = rest.astype(jnp.bfloat16)
+            g3 = (rest - g2.astype(jnp.float32)).astype(jnp.bfloat16)
+            at = pl.multiple_of(q * 16, 16)
+            gmat[r, pl.ds(at, 16), :] = g1
+            gmat[r, pl.ds(at + TOK, 16), :] = g2
+            gmat[r, pl.ds(at + 2 * TOK, 16), :] = g3
+            return 0
+        lax.fori_loop(0, 4 * (TOK // 16), rows, 0)
+
+    def partial(r, d):
+        w = o_buf[r, :, :, pl.ds(pl.multiple_of(d * COL, COL), COL)].reshape(slots, COL)
+        p = jnp.dot(gmat[r], w, preferred_element_type=jnp.float32)
+        return p[:TOK] + p[TOK:2 * TOK] + p[2 * TOK:]
+
+    def take_local(i):
+        d = i % n_col
+        d_copy(1, d).wait_recv()
+        acc[i] += drecv[1, d]
+        @pl.when(i // n_col < n_tok - 1)
+        def _():
+            pl.semaphore_signal(credit.at[1], inc=1, device_id={'ep': partner}, device_id_type=MESH)
+
+    def finish(j):
+        y_copy(j).wait_recv()
+        hz[j] = (acc[j] + yrecv[j]).astype(jnp.bfloat16)
+        z_copy(j).start()
+
+    def step(i, _):
+        c, d = i // n_col, i % n_col
+
+        @pl.when(d == 0)
+        def _():
+            build(c)
+
+        @pl.when(c == 0)
+        def _():
+            for r in range(4):
+                o_copy(r, d).wait()
+
+        @pl.when(c > 0)
+        def _():
+            for kind in range(2):
+                d_copy(kind, d).wait_send()
+                pl.semaphore_wait(credit.at[kind], 1)
+
+        dsend[0, d] = partial(0, d)
+        ysend[i] = partial(1, d)
+        d_copy(0, d).start()
+        dsend[1, d] = partial(2, d)
+        h_copy(i).wait()
+        acc[i] = partial(3, d) + hz[i].astype(jnp.float32)
+        d_copy(1, d).start()
+        d_copy(0, d).wait_recv()
+        ysend[i] += drecv[0, d]
+
+        @pl.when(c < n_tok - 1)
+        def _():
+            pl.semaphore_signal(credit.at[0], inc=1, device_id={'ep': partner}, device_id_type=MESH)
+
+        @pl.when(i > 0)
+        def _():
+            take_local(i - 1)
+
+        y_copy(i).start()
+
+        @pl.when((i >= 3) & (i % 2 == 1))
+        def _():
+            finish((i - 3) // 2)
+        return 0
+
+    lax.fori_loop(0, n_piece, step, 0)
+    take_local(n_piece - 1)
+
+    def tail(j, _):
+        finish(j)
+        return 0
+    lax.fori_loop((n_piece - 4) // 2 + 1, n_piece, tail, 0)
+
+    def arrive(i, _):
+        z_copy(i).wait_recv()
+        y_copy(i).wait_send()
+        z_copy(i).wait_send()
+        return 0
+    lax.fori_loop(0, n_piece, arrive, 0)
+    out = pltpu.make_async_copy(zrecv, out_hbm, out_sem)
+    out.start()
+    for d in range(n_col):
+        for kind in range(2):
+            d_copy(kind, d).wait_send()
+    for r in range(3):
+        t_copy(r).wait_send()
+    out.wait()
+
+
+def exchange(pp_size, expert_out, table, resid, ep_size):
+    experts, cap_all, width = expert_out.shape
+    tokens = resid.shape[0]
+    cap = cap_all // ep_size
+    n_tok, n_col = tokens // TOK, width // COL
+    n_piece = n_tok * n_col
+    dma = pltpu.SemaphoreType.DMA
+    return pl.pallas_call(
+        functools.partial(combine_kernel, pp_size),
+        out_shape=jax.ShapeDtypeStruct((n_tok, TOK, width), jnp.bfloat16),
+        in_specs=[pl.BlockSpec(memory_space=pl.ANY), pl.BlockSpec(memory_space=pltpu.VMEM), pl.BlockSpec(memory_space=pl.ANY)],
+        out_specs=pl.BlockSpec(memory_space=pl.ANY),
+        scratch_shapes=[
+            pltpu.VMEM((4, experts, cap, width), jnp.bfloat16),
+            pltpu.VMEM((3, 16, tokens), jnp.float32),
+            pltpu.VMEM((4, tokens, 16), jnp.float32),
+            pltpu.VMEM((4, 3 * TOK, experts * cap), jnp.bfloat16),
+            pltpu.VMEM((n_piece, TOK, COL), jnp.float32),
+            pltpu.VMEM((n_piece, TOK, COL), jnp.float32),
+            pltpu.VMEM((n_piece, TOK, COL), jnp.float32),
+            pltpu.VMEM((2, n_col, TOK, COL), jnp.float32),
+            pltpu.VMEM((2, n_col, TOK, COL), jnp.float32),
+            pltpu.VMEM((n_piece, TOK, COL), jnp.bfloat16),
+            pltpu.VMEM((n_tok, TOK, width), jnp.bfloat16),
+            dma((4, n_col)), dma((n_piece,)), dma((3,)), dma((3,)), dma((2, n_col)), dma((2, n_col)),
+            pltpu.SemaphoreType.REGULAR((2,)),
+            dma((n_piece,)), dma((n_piece,)), dma((n_piece,)), dma((n_piece,)), dma,
+        ],
+        compiler_params=pltpu.CompilerParams(collective_id=0, has_side_effects=True, vmem_limit_bytes=64 * 1000 * 1024),
+    )(expert_out, table, resid)
 
 
 def attn_block(merged, scale_vec, w_query, w_key, w_value, w_out):
@@ -29,22 +238,16 @@
 def solution(mesh):
     ep_size = mesh.shape['ep']
     pp_size = mesh.shape['pp']
-    next_stage = [(source, (source + 1) % pp_size) for source in range(pp_size)]
     token_spec = P(('data', 'pp'), 'ep', None, None)
     weight_spec = P('pp', None, None, None)
 
     def body(expert_out, expert_ids, slot_ids, gate_vals, residual, norm_scale, w_query, w_key, w_value, w_out):
         local_experts, capacity, model_width = expert_out.shape[1:]
         cap_dev = capacity // ep_size
-        send_buf = expert_out[0].reshape(local_experts, ep_size, cap_dev, model_width)
-        received = lax.all_to_all(send_buf, 'ep', 1, 0, tiled=True).reshape(-1, model_width)
-        kept_mask = slot_ids[0] >= 0
-        local_slot = slot_ids[0] - lax.axis_index('ep') * cap_dev
-        row_ids = jnp.where(kept_mask, expert_ids[0] * cap_dev + local_slot, 0)
-        gate_used = jnp.where(kept_mask, gate_vals[0], 0.0)
-        picked_rows = jnp.take(received, row_ids, axis=0)
-        merged = (residual[0].astype(jnp.float32) + jnp.sum(picked_rows * gate_used[..., None], axis=-2)).astype(jnp.bfloat16)
-        arrived = lax.ppermute(merged, 'pp', next_stage)
+        ids, slots, gates = (jnp.swapaxes(a[0, 0], 0, 1) for a in (expert_ids, slot_ids, gate_vals))
+        key = jnp.where(slots >= 0, ids * cap_dev + slots - lax.axis_index('ep') * cap_dev, -1)
+        table = jnp.concatenate([key.astype(jnp.float32), gates], axis=0)
+        arrived = exchange(pp_size, expert_out[0], table, residual[0, 0], ep_size).reshape(1, -1, model_width)
         result = attn_block(arrived, norm_scale[0], w_query[0], w_key[0], w_value[0], w_out[0])
         return result[None]
 

time: 426 us -> 183 us (0.43)
  waiting for transfers between devices: 275 us -> 0 us
  Pallas kernels: 0 us -> 117 us
  local copies, waits for them, and re-layouts: 59.2 us -> 0.01 us
  other arithmetic: 28.3 us -> 15.6 us
  starting transfers between devices: 10.5 us -> 0 us
    all_to_all x1 -> x0, waiting for transfers between devices: 228 us -> none  [body(): lax.all_to_all(send_buf, 'ep', 1, 0, tiled=True).reshape(-1, model_width)]
    pallas_call x0 -> x1, Pallas kernels: none -> 117 us  [exchange(): pl.pallas_call(functools.partial(combine_kernel, pp_size), out_shape=jax....]
    ppermute x1 -> x0, waiting for transfers between devices: 47.8 us -> none  [body(): arrived = lax.ppermute(merged, 'pp', next_stage)]
    gather x1 -> x0, local copies, waits for them, and re-layouts: 41 us -> none  [body(): picked_rows = jnp.take(received, row_ids, axis=0)]
    reduce_sum x1 -> x0, other arithmetic: 17.7 us -> none  [body(): jnp.sum(picked_rows * gate_used[..., None], axis=-2)]
    another operation x1 -> x0, local copies, waits for them, and re-layouts: 17.6 us -> none  [body(): expert_out[0].reshape(local_experts, ep_size, cap_dev, model_width)]
    all_to_all x1 -> x0, starting transfers between devices: 7.85 us -> none  [body(): lax.all_to_all(send_buf, 'ep', 1, 0, tiled=True).reshape(-1, model_width)]
  transfers between devices with their start and end apart: 2 -> 0, of which waited for: 2 -> 0; matrix products, arithmetic and copies ran while one was open for 0% -> 0% of each run, Pallas kernels for 0% -> 0%
where the time goes in v1:
time: 183 us; the launch traced here: 182 us
  Pallas kernels  117 us (64%)
  matrix products  49.7 us (27%)
  other arithmetic  15.6 us (9%)
    pallas_call x1, Pallas kernels, exchange(): pl.pallas_call(functools.partial(combine_kernel, pp_size), out_shape=jax....  117 us
    dot_general x1, matrix products, attn_block(): jnp.einsum('crif,ife->cre', attn_out, w_out, preferred_element_type=jnp.f...  16.2 us
    dot_general x1, matrix products, attn_block(): jnp.einsum('bqhe,bkhe->bhqk', q_heads, k_heads, preferred_element_type=jn...  13.2 us
    dot_general x1, matrix products, attn_block(): jnp.einsum('bld,dhe->blhe', normed_in, w_value, preferred_element_type=jn...  10.5 us
    dot_general x1, matrix products, attn_block(): jnp.einsum('bld,dhe->blhe', normed_in, w_query, preferred_element_type=jn...  9.87 us
    reduce_sum x1, other arithmetic, attn_block(): row_sums = jnp.sum(exp_scores, axis=-1)  9.19 us

profile of v1, /device:TPU:0, one launch (start us, length us, event | category | flops | bytes accessed | tf_op | source)
XLA Modules:
  0.0 182.1 jit_solution(2518139908999889694)
XLA Ops:
  0.0 0.7 convert_bitcast_fusion
  0.7 1.3 pad_maximum_fusion.tbl_in
  2.1 0.0 copy-start.2
  2.1 116.7 %shard_map.100 = bf16[4,128,2048]{2,1,0:T(8,128)(2,1)} custom-call(bf16[16,320,2048]{2,1,0:T(8,128)(2,1)} %bitcast.62, f32[16,512]{1,0:T(8,128)} %pad_maximum_fusion.tbl_in, bf16[512,2048]{1,0:T(8,128)(2,1)} %bitcast.63), custom_call_target="tpu_custom_call" | custom-call | tf_op jit(solution)/shard_map/pallas_call | solution.py:193
  118.8 2.1 %multiply_reduce_fusion = f32[4,128]{1,0:T(4,128)S(1)} fusion(bf16[4,128,2048]{2,1,0:T(8,128)(2,1)} %shard_map.100), kind=kLoop, calls=%fused_computation.24 | loop fusion | flops 3145216 | bytes 2099200 | tf_op jit(solution)/shard_map/reduce_sum | solution.py:222
  120.9 0.0 copy-done.2
  120.9 2.1 %multiply_convert_fusion = bf16[4,128,2048]{2,1,0:T(8,128)(2,1)S(1)} fusion(bf16[4,128,2048]{2,1,0:T(8,128)(2,1)} %shard_map.100, f32[2048]{0:T(1024)S(1)} %bitcast.69, f32[4,128]{1,0:T(4,128)S(1)} %add_rsqrt_fusion), kind=kLoop, calls=%fused_computation.23 | loop fusion | flops 4194304 | bytes 4204544 | tf_op jit(solution)/shard_map/convert_element_type | solution.py:223
  123.1 0.0 copy-start.1
  123.1 9.9 %fusion.9 = bf16[512,16,128]{2,0,1:T(8,128)(2,1)} fusion(bf16[512,2048,1]{1,0,2:T(8,128)(2,1)S(1)} %bitcast.64, bf16[2048,16,128]{2,1,0:T(8,128)(2,1)} %bitcast.70), kind=kOutput, calls=%fused_computation.10 | convolution fusion | flops 4294967296 | bytes 12582912 | tf_op jit(solution)/shard_map/bld,dhe->blhe/dot_general | solution.py:224
  132.9 0.1 iota_compare_fusion
  133.0 0.0 copy-done.1
  133.0 13.2 %fusion = (f32[16,512]{1,0:T(8,128)S(1)}, f32[16,512,512]{1,2,0:T(8,128)}) fusion(pred[512,512]{0,1:T(8,128)(4,1)S(1)} %iota_compare_fusion, bf16[512,16,128]{2,0,1:T(8,128)(2,1)} %fusion.9, bf16[512,2048,1]{1,0,2:T(8,128)(2,1)S(1)} %bitcast.65, bf16[2048,16,128]{2,1,0:T(8,128)(2,1)} %bitcast.71), kind=kOutput, calls=%fused_computation.2 | convolution fusion | flops 5382332416 | bytes 29655040 | tf_op jit(solution)/shard_map/bqhe,bkhe->bhqk/dot_general | solution.py:227
  146.2 9.2 %fusion.1 = f32[16,512]{1,0:T(8,128)S(1)} fusion(f32[16,512,512]{1,2,0:T(8,128)} %get-tuple-element.6, f32[16,512]{1,0:T(8,128)S(1)} %get-tuple-element.5, pred[512,512]{0,1:T(8,128)(4,1)S(1)} %iota_compare_fusion), kind=kLoop, calls=%fused_computation.3 | loop fusion | flops 16769024 | bytes 17104896 | tf_op jit(solution)/shard_map/reduce_sum | solution.py:231
  155.4 0.0 copy-start
  155.4 10.5 %fusion.11 = bf16[512,16,128]{0,2,1:T(8,128)(2,1)} fusion(bf16[512,2048,1]{1,0,2:T(8,128)(2,1)} %bitcast.66, bf16[2048,16,128]{2,1,0:T(8,128)(2,1)} %bitcast.72), kind=kOutput, calls=%fused_computation.12 | convolution fusion | flops 4294967296 | bytes 12582912 | tf_op jit(solution)/shard_map/bld,dhe->blhe/dot_general | solution.py:226
  165.9 0.0 copy-done
  165.9 16.2 %fusion.23 = bf16[1,1,512,2048]{3,2,1,0:T(8,128)(2,1)} fusion(bf16[1,16,128,2048]{3,2,1,0:T(8,128)(2,1)} %param.19, f32[16,512,512]{1,2,0:T(8,128)} %get-tuple-element.6, f32[16,512]{1,0:T(8,128)S(1)} %get-tuple-element.5, pred[512,512]{0,1:T(8,128)(4,1)S(1)} %iota_compare_fusion, bf16[4,128,2048]{2,1,0:T(8,128)(2,1)S(1)} %copy-done, ...), kind=kOutput, calls=%fused_computation.25 | convolution fusion | flops 5392826368 | bytes 31784960 | tf_op jit(solution)/shard_map/crif,ife->cre/dot_general | solution.py:234
  (1 shorter events, 0.0 us)
Async XLA Ops:
  2.1 118.8 %copy-start.2 = (f32[1,2048]{1,0:T(1,128)S(1)}, f32[1,2048]{1,0:T(1,128)}, u32[]{:S(2)}) copy-start(f32[1,2048]{1,0:T(1,128)} %param.15) | copy-start | bytes 24580
  123.1 10.0 %copy-start.1 = (bf16[4,128,2048]{2,1,0:T(8,128)(2,1)}, bf16[4,128,2048]{2,1,0:T(8,128)(2,1)S(1)}, u32[]{:S(2)}) copy-start(bf16[4,128,2048]{2,1,0:T(8,128)(2,1)S(1)} %multiply_convert_fusion) | copy-start | bytes 6291460
  155.4 10.5 %copy-start = (bf16[4,128,2048]{2,1,0:T(8,128)(2,1)S(1)}, bf16[4,128,2048]{2,1,0:T(8,128)(2,1)}, u32[]{:S(2)}) copy-start(bf16[4,128,2048]{2,1,0:T(8,128)(2,1)} %shard_map.100) | copy-start | bytes 6291460

commit v2 on v1

v2 whole, which is shorter than its diff:
```python
import functools

import jax
import jax.numpy as jnp
from jax import lax
from jax.experimental import pallas as pl
from jax.experimental.pallas import tpu as pltpu
from jax.sharding import PartitionSpec as P

NORM_EPS = 1e-6
MESH = pl.DeviceIdType.MESH
TOK = 128
COL = 512
BLK = 128
NSLOT = 2


def stage_kernel(pp_size, heads, o_hbm, ids_in, slot_in, gate_in, h_hbm, scale_in, wq_hbm, wk_hbm, wv_hbm, wo_hbm, out_hbm,
                 arena, tids, tslot, tgate, tblt, gmat, ysend, acc, yrecv, dsend, drecv, hz, zrecv, stage_buf, wo_buf, qbuf, kbuf, vbuf, xbuf,
                 o_sem, h_sem, t_ssem, t_rsem, d_ssem, d_rsem, credit, y_ssem, y_rsem, z_ssem, z_rsem, s_sem, w_sem, out_sem):
    experts, cap_all, width = o_hbm.shape
    cap = cap_all // 4
    slots = experts * cap
    tokens = h_hbm.shape[0]
    head_dim = width // heads
    n_tok, n_col = tokens // TOK, width // COL
    n_piece = n_tok * n_col
    me = lax.axis_index('ep')
    core = lax.rem(me, 2)
    row = me // 2
    partner = row * 2 + (1 - core)
    peer = (1 - row) * 2 + core
    diag = (1 - row) * 2 + (1 - core)
    owners = (diag, peer, partner, me)
    stage = lax.axis_index('pp')
    nxt = lax.rem(stage + 1, pp_size)
    prv = lax.rem(stage + pp_size - 1, pp_size)

    def o_start(r, d):
        def one(e, _):
            pltpu.make_async_copy(o_hbm.at[e, pl.ds(owners[r] * cap, cap), pl.ds(d * COL, COL)],
                                  arena.at[pl.ds(pl.multiple_of(r * slots + e * cap, 16), cap), pl.ds(d * COL, COL)], o_sem.at[r, d]).start()
            return 0
        lax.fori_loop(0, experts, one, 0)

    def o_wait(r, d):
        view = arena.at[pl.ds(r * slots, slots), pl.ds(pl.multiple_of(d * COL, COL), COL)]
        pltpu.make_async_copy(view, view, o_sem.at[r, d]).wait()

    def h_copy(i):
        c, d = i // n_col, i % n_col
        return pltpu.make_async_copy(h_hbm.at[pl.ds(c * TOK, TOK), pl.ds(d * COL, COL)], hz.at[i], h_sem.at[i])

    tables = ((ids_in, tids), (slot_in, tslot), (gate_in, tgate))

    def t_copy(k, r):
        return pltpu.make_async_remote_copy(src_ref=tables[k][0], dst_ref=tables[k][1].at[r], send_sem=t_ssem.at[k, r],
                                            recv_sem=t_rsem.at[k, r], device_id={'ep': owners[r]}, device_id_type=MESH)

    def d_copy(kind, i):
        at = i % NSLOT
        return pltpu.make_async_remote_copy(src_ref=dsend.at[kind, at], dst_ref=drecv.at[kind, at], send_sem=d_ssem.at[kind, at],
                                            recv_sem=d_rsem.at[kind, at], device_id={'ep': partner}, device_id_type=MESH)

    def y_copy(i):
        return pltpu.make_async_remote_copy(src_ref=ysend.at[i], dst_ref=yrecv.at[i], send_sem=y_ssem.at[i], recv_sem=y_rsem.at[i],
                                            device_id={'ep': peer}, device_id_type=MESH)

    def z_copy(i):
        c, d = i // n_col, i % n_col
        return pltpu.make_async_remote_copy(src_ref=hz.at[i], dst_ref=zrecv.at[c, :, pl.ds(pl.multiple_of(d * COL, COL), COL)],
                                            send_sem=z_ssem.at[i], recv_sem=z_rsem.at[i], device_id={'pp': nxt}, device_id_type=MESH)

    raw = (wq_hbm, wk_hbm, wv_hbm)

    def s_copy(w, b):
        at = b % 2
        return pltpu.make_async_copy(raw[w].at[pl.ds(b * BLK, BLK)], stage_buf.at[at], s_sem.at[at])

    def w_copy(n):
        at = n % 2
        return pltpu.make_async_copy(wo_hbm.at[:, pl.ds(pl.multiple_of(n * COL, COL), COL)], wo_buf.at[at], w_sem.at[at])

    for r in range(4):
        o_start(r, 0)

    barrier = pltpu.get_barrier_semaphore()
    for dev in (partner, peer, diag):
        pl.semaphore_signal(barrier, inc=1, device_id={'ep': dev}, device_id_type=MESH)
    for dev in (nxt, prv):
        pl.semaphore_signal(barrier, inc=1, device_id={'pp': dev}, device_id_type=MESH)
    pl.semaphore_wait(barrier, 5)

    for r in range(3):
        for k in range(3):
            t_copy(k, r).start()

    def keyed(r, ids, slot, gate):
        key = jnp.where(slot >= 0, (ids - me * experts) * cap + (slot - owners[r] * cap), -1).astype(jnp.float32)
        tblt[r] = jnp.transpose(jnp.concatenate([key, gate], axis=0))

    keyed(3, ids_in[...], slot_in[...], gate_in[...])
    for r in range(3):
        for k in range(3):
            t_copy(k, r).wait_recv()
        keyed(r, tids[r], tslot[r], tgate[r])
    for d in range(1, n_col):
        for r in range(4):
            o_start(r, d)
    for i in range(n_piece):
        h_copy(i).start()
    s_copy(0, 0).start()
    w_copy(0).start()
    w_copy(1).start()

    groups = TOK // 16

    def build(c, first):
        def rows(k, _):
            r, q = first + k // groups, k % groups
            t = tblt[r, pl.ds(pl.multiple_of(c * TOK + q * 16, 16), 16), :]
            lane = lax.broadcasted_iota(jnp.int32, (16, slots), 1).astype(jnp.float32)
            g = jnp.zeros((16, slots), jnp.float32)
            for j in range(8):
                g = jnp.where(lane == t[:, j:j + 1], t[:, 8 + j:9 + j], g)
            g1 = g.astype(jnp.bfloat16)
            rest = g - g1.astype(jnp.float32)
            g2 = rest.astype(jnp.bfloat16)
            g3 = (rest - g2.astype(jnp.float32)).astype(jnp.bfloat16)
            at = pl.multiple_of(q * 16, 16)
            gmat[r, pl.ds(at, 16), :] = g1
            gmat[r, pl.ds(at + TOK, 16), :] = g2
            gmat[r, pl.ds(at + 2 * TOK, 16), :] = g3
            return 0
        lax.fori_loop(0, 2 * groups, rows, 0)

    def partial(r, d):
        w = arena[pl.ds(r * slots, slots), pl.ds(pl.multiple_of(d * COL, COL), COL)]
        p = jnp.dot(gmat[r], w, preferred_element_type=jnp.float32)
        return p[:TOK] + p[TOK:2 * TOK] + p[2 * TOK:]

    def give(kind, i):
        @pl.when(i < n_piece - NSLOT)
        def _():
            pl.semaphore_signal(credit.at[kind], inc=1, device_id={'ep': partner}, device_id_type=MESH)

    def take_local(i):
        d_copy(1, i).wait_recv()
        acc[i] += drecv[1, i % NSLOT]
        give(1, i)

    def finish(j):
        y_copy(j).wait_recv()
        hz[j] = (acc[j] + yrecv[j]).astype(jnp.bfloat16)
        z_copy(j).start()

    def step(i, _):
        c, d = i // n_col, i % n_col

        @pl.when(d == 0)
        def _():
            build(c, 0)

        @pl.when(c == 0)
        def _():
            for r in range(4):
                o_wait(r, d)

        @pl.when(i >= NSLOT)
        def _():
            for kind in range(2):
                d_copy(kind, i).wait_send()
                pl.semaphore_wait(credit.at[kind], 1)

        dsend[0, i % NSLOT] = partial(0, d)
        ysend[i] = partial(1, d)
        d_copy(0, i).start()

        @pl.when(d == 0)
        def _():
            build(c, 2)

        dsend[1, i % NSLOT] = partial(2, d)
        d_copy(0, i).wait_recv()
        ysend[i] += drecv[0, i % NSLOT]
        give(0, i)
        h_copy(i).wait()
        acc[i] = partial(3, d) + hz[i].astype(jnp.float32)
        y_copy(i).start()
        d_copy(1, i).start()

        @pl.when(i > 0)
        def _():
            take_local(i - 1)

        @pl.when((i >= 5) & (i % 2 == 1))
        def _():
            finish((i - 5) // 2)
        return 0

    lax.fori_loop(0, n_piece, step, 0)
    take_local(n_piece - 1)

    n_blk = width // BLK

    def relay(w):
        def block(b, _):
            at = b % 2
            s_copy(w, b).wait()

            @pl.when(b < n_blk - 1)
            def _():
                s_copy(w, b + 1).start()

            if w < 2:
                @pl.when(b == n_blk - 1)
                def _():
                    s_copy(w + 1, 0).start()

            def sub(k, _):
                rows = pl.multiple_of(k * 64, 64)
                arena[pl.ds(pl.multiple_of(w * width + b * BLK + rows, 64), 64), :] = stage_buf[at, pl.ds(rows, 64)].reshape(64, width)
                return 0
            lax.fori_loop(0, BLK // 64, sub, 0)
            return 0
        lax.fori_loop(0, n_blk, block, 0)

    def attend(c, hook):
        for d in range(n_col):
            z_copy(c * n_col + d).wait_recv()
        scale = scale_in[...]

        def norm(k, _):
            rows = pl.ds(pl.multiple_of(k * 16, 16), 16)
            x = zrecv[c, rows, :].astype(jnp.float32)
            inv = lax.rsqrt(jnp.mean(x * x, axis=-1, keepdims=True) + NORM_EPS)
            xbuf[rows, :] = (x * inv * scale).astype(jnp.bfloat16)
            return 0
        lax.fori_loop(0, TOK // 16, norm, 0)

        def project(n, _):
            cols = pl.ds(pl.multiple_of(n * COL, COL), COL)
            x = xbuf[...]
            qbuf[:, cols] = jnp.dot(x, arena[0:width, cols], preferred_element_type=jnp.float32).astype(jnp.bfloat16)
            kbuf[c * TOK:(c + 1) * TOK, cols] = jnp.dot(x, arena[width:2 * width, cols], preferred_element_type=jnp.float32).astype(jnp.bfloat16)
            vbuf[c * TOK:(c + 1) * TOK, cols] = jnp.dot(x, arena[2 * width:3 * width, cols], preferred_element_type=jnp.float32).astype(jnp.bfloat16)
            return 0
        lax.fori_loop(0, n_col, project, 0)
        hook(0)
        seen = (c + 1) * TOK
        q_at = lax.broadcasted_iota(jnp.int32, (TOK, seen), 0) + c * TOK
        k_at = lax.broadcasted_iota(jnp.int32, (TOK, seen), 1)
        causal = q_at >= k_at

        def head(h, _):
            for u in range(2):
                cols = pl.ds(pl.multiple_of((h * 2 + u) * head_dim, head_dim), head_dim)
                s = lax.dot_general(qbuf[:, cols], kbuf[0:seen, cols], (((1,), (1,)), ((), ())), preferred_element_type=jnp.float32)
                s = jnp.where(causal, s * (head_dim ** -0.5), -1e30)
                p = jnp.exp(s - jnp.max(s, axis=-1, keepdims=True))
                total = jnp.sum(p, axis=-1, keepdims=True)
                mixed = jnp.dot(p.astype(jnp.bfloat16), vbuf[0:seen, cols], preferred_element_type=jnp.float32)
                xbuf[:, cols] = (mixed / total).astype(jnp.bfloat16)
            return 0
        lax.fori_loop(0, heads // 2, head, 0)
        hook(1)

        def output(n, _):
            cols = pl.ds(pl.multiple_of(n * COL, COL), COL)
            w_copy(n).wait()
            proj = jnp.dot(xbuf[...], wo_buf[n % 2], preferred_element_type=jnp.float32).astype(jnp.bfloat16)
            zrecv[c, :, cols] = (zrecv[c, :, cols].astype(jnp.float32) + proj.astype(jnp.float32)).astype(jnp.bfloat16)
            if c < n_tok - 1:
                w_copy((n + 2) % n_col).start()
            else:
                @pl.when(n < n_col - 2)
                def _():
                    w_copy(n + 2).start()
            return 0
        lax.fori_loop(0, n_col, output, 0)
        pltpu.make_async_copy(zrecv.at[c], out_hbm.at[c], out_sem.at[c]).start()
        hook(2)

    relay(0)
    finish(6)
    relay(1)
    finish(7)
    relay(2)
    plan = {(0, 0): (8,), (0, 2): (9,), (1, 0): (10,), (1, 2): (11, 12), (2, 0): (13,), (2, 2): (14, 15)}
    for c in range(n_tok):
        def hook(at, c=c):
            for j in plan.get((c, at), ()):
                finish(j)
        attend(c, hook)

    def drain(i, _):
        y_copy(i).wait_send()
        z_copy(i).wait_send()
        return 0
    lax.fori_loop(0, n_piece, drain, 0)
    for i in range(NSLOT):
        for kind in range(2):
            d_copy(kind, i).wait_send()
    for r in range(3):
        for k in range(3):
            t_copy(k, r).wait_send()
    for c in range(n_tok):
        pltpu.make_async_copy(zrecv.at[c], out_hbm.at[c], out_sem.at[c]).wait()


def run_stage(pp_size, expert_out, ids, slot, gate, resid, scale, wq, wk, wv, wo):
    experts, cap_all, width = expert_out.shape
    tokens = resid.shape[0]
    heads = wq.shape[1]
    slots = experts * cap_all // 4
    n_tok, n_col = tokens // TOK, width // COL
    n_piece = n_tok * n_col
    dma = pltpu.SemaphoreType.DMA
    anyspace = pl.BlockSpec(memory_space=pl.ANY)
    vmem = pl.BlockSpec(memory_space=pltpu.VMEM)
    f32, bf16 = jnp.float32, jnp.bfloat16
    return pl.pallas_call(
        functools.partial(stage_kernel, pp_size, heads),
        out_shape=jax.ShapeDtypeStruct((n_tok, TOK, width), bf16),
        in_specs=[anyspace, vmem, vmem, vmem, anyspace, vmem, anyspace, anyspace, anyspace, anyspace],
        out_specs=anyspace,
        scratch_shapes=[
            pltpu.VMEM((max(4 * slots, 3 * width), width), bf16),
            pltpu.VMEM((3, 8, tokens), jnp.int32), pltpu.VMEM((3, 8, tokens), jnp.int32), pltpu.VMEM((3, 8, tokens), f32),
            pltpu.VMEM((4, tokens, 16), f32),
            pltpu.VMEM((4, 3 * TOK, slots), bf16),
            pltpu.VMEM((n_piece, TOK, COL), f32), pltpu.VMEM((n_piece, TOK, COL), f32), pltpu.VMEM((n_piece, TOK, COL), f32),
            pltpu.VMEM((2, NSLOT, TOK, COL), f32), pltpu.VMEM((2, NSLOT, TOK, COL), f32),
            pltpu.VMEM((n_piece, TOK, COL), bf16),
            pltpu.VMEM((n_tok, TOK, width), bf16),
            pltpu.VMEM((2, BLK, heads, width // heads), bf16),
            pltpu.VMEM((2, width, COL), bf16),
            pltpu.VMEM((TOK, width), bf16), pltpu.VMEM((tokens, width), bf16), pltpu.VMEM((tokens, width), bf16), pltpu.VMEM((TOK, width), bf16),
            dma((4, n_col)), dma((n_piece,)), dma((3, 3)), dma((3, 3)), dma((2, NSLOT)), dma((2, NSLOT)),
            pltpu.SemaphoreType.REGULAR((2,)),
            dma((n_piece,)), dma((n_piece,)), dma((n_piece,)), dma((n_piece,)), dma((2,)), dma((2,)), dma((n_tok,)),
        ],
        compiler_params=pltpu.CompilerParams(collective_id=0, has_side_effects=True, vmem_limit_bytes=67043328),
    )(expert_out, ids, slot, gate, resid, scale, wq, wk, wv, wo)


def solution(mesh):
    pp_size = mesh.shape['pp']
    token_spec = P(('data', 'pp'), 'ep', None, None)
    weight_spec = P('pp', None, None, None)

    def body(expert_out, expert_ids, slot_ids, gate_vals, residual, norm_scale, w_query, w_key, w_value, w_out):
        ids, slot, gate = (jnp.swapaxes(a[0, 0], 0, 1) for a in (expert_ids, slot_ids, gate_vals))
        width = expert_out.shape[-1]
        result = run_stage(pp_size, expert_out[0], ids, slot, gate, residual[0, 0], norm_scale, w_query[0], w_key[0], w_value[0], w_out[0].reshape(-1, width))
        return result.reshape(residual.shape)

    return jax.shard_map(body, mesh=mesh, in_specs=(token_spec, token_spec, token_spec, token_spec, token_spec, P('pp', None), weight_spec, weight_spec, weight_spec, weight_spec), out_specs=token_spec, check_vma=False)
```

time: 183 us -> 206 us (1.13)
  Pallas kernels: 117 us -> 201 us
  matrix products: 49.7 us -> 0 us
  other arithmetic: 15.6 us -> 0 us
  local copies, waits for them, and re-layouts: 0.01 us -> 3.16 us
    pallas_call x1, Pallas kernels: 117 us -> 201 us  [run_stage(): pl.pallas_call(functools.partial(stage_kernel, pp_size, heads), out_shape...]
    dot_general x4 -> x0, matrix products: 49.7 us -> none  [the longest x1 16.2 us: attn_block(): jnp.einsum('crif,ife->cre', attn_out, w_out, preferred_element_type=jnp.f...]
    reduce_sum x2 -> x0, other arithmetic: 11.3 us -> none  [the longest x1 9.19 us: attn_block(): row_sums = jnp.sum(exp_scores, axis=-1)]
    unnamed x6 -> x1, local copies, waits for them, and re-layouts: 0.01 us -> 3.16 us
    convert_element_type x2 -> x0, other arithmetic: 2.87 us -> none  [the longest x1 2.13 us: attn_block(): normed_in = (resid_f32 * inv_rms * scale_vec).astype(jnp.bfloat16)]
where the time goes in v2:
time: 206 us; the launch traced here: 204 us
  Pallas kernels  201 us (98%)
  local copies, waits for them, and re-layouts  3.16 us (2%)
    pallas_call x1, Pallas kernels, run_stage(): pl.pallas_call(functools.partial(stage_kernel, pp_size, heads), out_shape...  201 us

profile of v2, /device:TPU:0, one launch (start us, length us, event | category | flops | bytes accessed | tf_op | source)
XLA Modules:
  0.0 203.7 jit_solution(13151996243979330523)
XLA Ops:
  0.0 200.5 %shard_map.100 = bf16[4,128,2048]{2,1,0:T(8,128)(2,1)} custom-call(bf16[16,320,2048]{2,1,0:T(8,128)(2,1)} %bitcast.16, s32[8,512]{1,0:T(8,128)} %bitcast.23, s32[8,512]{1,0:T(8,128)} %bitcast.24, f32[8,512]{1,0:T(8,128)} %bitcast.25, bf16[512,2048]{1,0:T(8,128)(2,1)} %bitcast.22, f32[1,2048]{1,0:T(1,128)} %scale_in.1, bf16[2048,16,128]{2,1,0:T(8,128)(2,1)} %bitcast.18, ...), custom_call_target="tpu_custom_call" | custom-call | tf_op jit(solution)/shard_map/pallas_call | solution.py:322
  200.5 3.2 %copy.12 = bf16[1,1,512,2048]{3,2,1,0:T(8,128)(2,1)} copy(bf16[1,1,512,2048]{3,2,1,0:T(8,128)(2,1)} %bitcast.17) | data formatting | bytes 4194304

commit v3 on v2

v3 whole, which is shorter than its diff:
```python
import functools

import jax
import jax.numpy as jnp
from jax import lax
from jax.experimental import pallas as pl
from jax.experimental.pallas import tpu as pltpu
from jax.sharding import PartitionSpec as P

NORM_EPS = 1e-6
MESH = pl.DeviceIdType.MESH
TOK = 128
COL = 512
WIDE = 1024
BLK = 128
STAGED = 6
OUT = 256
WSLOT = 6
GROUP = 8


def stage_kernel(pp_size, heads, o_hbm, ids_in, slot_in, gate_in, h_hbm, scale_in, wq_hbm, wk_hbm, wv_hbm, wo_hbm, out_hbm,
                 arena, tids, tslot, tgate, tblt, gate_a, gate_b, ysend, acc, yrecv, dsend, drecv, hz, zrecv, stage_buf, wo_buf, qbuf, kbuf, vbuf, xbuf,
                 o_sem, h_sem, t_ssem, t_rsem, d_ssem, d_rsem, credit, y_ssem, y_rsem, z_ssem, z_rsem, s_sem, w_sem, out_sem):
    experts, cap_all, width = o_hbm.shape
    cap = cap_all // 4
    slots = experts * cap
    tokens = h_hbm.shape[0]
    head_dim = width // heads
    n_tok, n_col = tokens // TOK, width // COL
    n_piece = n_tok * n_col
    n_out = width // OUT
    gates = (gate_b, gate_a)
    me = lax.axis_index('ep')
    core = lax.rem(me, 2)
    row = me // 2
    partner = row * 2 + (1 - core)
    peer = (1 - row) * 2 + core
    diag = (1 - row) * 2 + (1 - core)
    owners = (diag, peer, partner, me)
    stage = lax.axis_index('pp')
    nxt = lax.rem(stage + 1, pp_size)
    prv = lax.rem(stage + pp_size - 1, pp_size)

    def o_start(r):
        def one(e, _):
            pltpu.make_async_copy(o_hbm.at[e, pl.ds(owners[r] * cap, cap)],
                                  arena.at[pl.ds(pl.multiple_of(r * slots + e * cap, 16), cap)], o_sem.at[r]).start()
            return 0
        lax.fori_loop(0, experts, one, 0)

    def o_wait(r):
        view = arena.at[pl.ds(r * slots, slots)]
        pltpu.make_async_copy(view, view, o_sem.at[r]).wait()

    def h_copy(i):
        c, d = i // n_col, i % n_col
        return pltpu.make_async_copy(h_hbm.at[pl.ds(c * TOK, TOK), pl.ds(d * COL, COL)], hz.at[i], h_sem.at[i])

    tables = ((ids_in, tids), (slot_in, tslot), (gate_in, tgate))

    def t_copy(k, r):
        return pltpu.make_async_remote_copy(src_ref=tables[k][0], dst_ref=tables[k][1].at[r], send_sem=t_ssem.at[k, r],
                                            recv_sem=t_rsem.at[k, r], device_id={'ep': owners[r]}, device_id_type=MESH)

    def d_copy(d):
        return pltpu.make_async_remote_copy(src_ref=dsend.at[d], dst_ref=drecv.at[d], send_sem=d_ssem.at[d],
                                            recv_sem=d_rsem.at[d], device_id={'ep': partner}, device_id_type=MESH)

    def y_copy(i):
        return pltpu.make_async_remote_copy(src_ref=ysend.at[i], dst_ref=yrecv.at[i], send_sem=y_ssem.at[i], recv_sem=y_rsem.at[i],
                                            device_id={'ep': peer}, device_id_type=MESH)

    def z_copy(i):
        c, d = i // n_col, i % n_col
        return pltpu.make_async_remote_copy(src_ref=hz.at[i], dst_ref=zrecv.at[c, :, pl.ds(pl.multiple_of(d * COL, COL), COL)],
                                            send_sem=z_ssem.at[i], recv_sem=z_rsem.at[i], device_id={'pp': nxt}, device_id_type=MESH)

    raw = (wq_hbm, wk_hbm, wv_hbm)

    n_blk = width // BLK

    def s_copy(w, b, at):
        return pltpu.make_async_copy(raw[w].at[pl.ds(b * BLK, BLK)], stage_buf.at[at], s_sem.at[at])

    def s_start(m):
        for w in range(3):
            @pl.when(m // n_blk == w)
            def _():
                s_copy(w, m % n_blk, m % STAGED).start()

    def w_copy(n):
        at = n % WSLOT
        return pltpu.make_async_copy(wo_hbm.at[:, pl.ds(pl.multiple_of(n % n_out * OUT, OUT), OUT)], wo_buf.at[at], w_sem.at[at])

    def keyed(r, ids, slot, gate):
        key = jnp.where(slot >= 0, (ids - me * experts) * cap + (slot - owners[r] * cap), -1).astype(jnp.float32)
        tblt[:, r * 16:(r + 1) * 16] = jnp.transpose(jnp.concatenate([key, gate], axis=0))

    groups = TOK // 16

    def build(c, r, q):
        t = tblt[pl.ds(pl.multiple_of(c * TOK + q * 16, 16), 16), r * 16:(r + 1) * 16]
        lane = lax.broadcasted_iota(jnp.int32, (16, slots), 1).astype(jnp.float32)
        g = jnp.zeros((16, slots), jnp.float32)
        for j in range(8):
            g = jnp.where(lane == t[:, j:j + 1], t[:, 8 + j:9 + j], g)
        g1 = g.astype(jnp.bfloat16)
        rest = g - g1.astype(jnp.float32)
        g2 = rest.astype(jnp.bfloat16)
        g3 = (rest - g2.astype(jnp.float32)).astype(jnp.bfloat16)
        at = pl.multiple_of(q * 16, 16)
        dst = gates[r % 2]
        dst[pl.ds(at, 16), :] = g1
        dst[pl.ds(at + TOK, 16), :] = g2
        dst[pl.ds(at + 2 * TOK, 16), :] = g3

    def build_all(c, r):
        def one(q, _):
            build(c, r, q)
            return 0
        lax.fori_loop(0, groups, one, 0)

    halves = width // WIDE
    per = WIDE // COL

    def phase(c, r, ahead, before, use):
        def half(h, _):
            before(h)
            w = arena[r * slots:(r + 1) * slots, pl.ds(pl.multiple_of(h * WIDE, WIDE), WIDE)]
            p = jnp.dot(gates[r % 2][...], w, preferred_element_type=jnp.float32)
            total = p[:TOK] + p[TOK:2 * TOK] + p[2 * TOK:]
            if ahead is not None:
                for q in range(groups // halves):
                    build(*ahead, h * (groups // halves) + q)
            for u in range(per):
                use(h * per + u, total[:, u * COL:(u + 1) * COL])
            return 0
        lax.fori_loop(0, halves, half, 0)

    def give():
        pl.semaphore_signal(credit, inc=1, device_id={'ep': partner}, device_id_type=MESH)

    def hold(d):
        d_copy(d).wait_send()
        pl.semaphore_wait(credit, 1)

    def send_core(d, value):
        dsend[d] = value
        d_copy(d).start()

    def self_role(c, ahead):
        def before(h):
            for u in range(per):
                h_copy(c * n_col + h * per + u).wait()

        def use(d, value):
            i = c * n_col + d
            acc[i] = value + hz[i].astype(jnp.float32)
        phase(c, 3, ahead, before, use)

    def take_local(c):
        def one(d, _):
            d_copy(d).wait_recv()
            acc[c * n_col + d] += drecv[d]

            @pl.when(c < n_tok - 1)
            def _():
                give()
            return 0
        lax.fori_loop(0, n_col, one, 0)

    def finish(j):
        y_copy(j).wait_recv()
        hz[j] = (acc[j] + yrecv[j]).astype(jnp.bfloat16)
        z_copy(j).start()

    o_start(3)
    o_start(0)
    barrier = pltpu.get_barrier_semaphore()
    for dev in (partner, peer, diag):
        pl.semaphore_signal(barrier, inc=1, device_id={'ep': dev}, device_id_type=MESH)
    for dev in (nxt, prv):
        pl.semaphore_signal(barrier, inc=1, device_id={'pp': dev}, device_id_type=MESH)
    for i in range(n_col):
        h_copy(i).start()
    keyed(3, ids_in[...], slot_in[...], gate_in[...])
    pl.semaphore_wait(barrier, 5)
    for r in range(3):
        for k in range(3):
            t_copy(k, r).start()
    build_all(0, 3)
    o_start(1)
    o_start(2)
    o_wait(3)
    self_role(0, None)
    for r in range(3):
        for k in range(3):
            t_copy(k, r).wait_recv()
        keyed(r, tids[r], tslot[r], tgate[r])
    build_all(0, 0)
    for r in range(3):
        o_wait(r)

    def rest_h(i, _):
        h_copy(i).start()
        return 0
    lax.fori_loop(n_col, n_piece, rest_h, 0)
    for m in range(STAGED - 1):
        s_copy(0, m, m).start()
    for n in range(WSLOT):
        w_copy(n).start()

    def chunk(c, _):
        def hold0(h):
            @pl.when(c > 0)
            def _():
                for u in range(per):
                    hold(h * per + u)
        phase(c, 0, (c, 1), hold0, send_core)

        def got(h):
            for u in range(per):
                d_copy(h * per + u).wait_recv()

        def merge(d, value):
            i = c * n_col + d
            ysend[i] = value + drecv[d]
            give()
            y_copy(i).start()
        phase(c, 1, (c, 2), got, merge)

        def hold2(h):
            for u in range(per):
                hold(h * per + u)
        phase(c, 2, (lax.rem(c + 1, n_tok), 3), hold2, send_core)

        @pl.when(c < n_tok - 1)
        def _():
            self_role(c + 1, (c + 1, 0))
        take_local(c)

        @pl.when(c > 0)
        def _():
            finish(2 * c - 2)
            finish(2 * c - 1)
        return 0

    with jax.named_scope('combine'):
        lax.fori_loop(0, n_tok, chunk, 0)

    def relay(w):
        def block(b, _):
            m = w * n_blk + b
            at = m % STAGED
            s_copy(w, b, at).wait()

            @pl.when(m + STAGED - 1 < 3 * n_blk)
            def _():
                s_start(m + STAGED - 1)

            def sub(k, _):
                rows = pl.multiple_of(k * 64, 64)
                arena[pl.ds(pl.multiple_of(w * width + b * BLK + rows, 64), 64), :] = stage_buf[at, pl.ds(rows, 64)].reshape(64, width)
                return 0
            lax.fori_loop(0, BLK // 64, sub, 0)
            return 0
        lax.fori_loop(0, n_blk, block, 0)

    def attend(c, hook):
        with jax.named_scope('zwait'):
            for d in range(n_col):
                z_copy(c * n_col + d).wait_recv()
        scale = scale_in[...]

        def norm(k, _):
            rows = pl.ds(pl.multiple_of(k * 16, 16), 16)
            x = zrecv[c, rows, :].astype(jnp.float32)
            inv = lax.rsqrt(jnp.mean(x * x, axis=-1, keepdims=True) + NORM_EPS)
            xbuf[rows, :] = (x * inv * scale).astype(jnp.bfloat16)
            return 0
        lax.fori_loop(0, TOK // 16, norm, 0)

        def project(n, _):
            cols = pl.ds(pl.multiple_of(n * COL, COL), COL)
            x = xbuf[...]
            qbuf[:, cols] = jnp.dot(x, arena[0:width, cols], preferred_element_type=jnp.float32).astype(jnp.bfloat16)
            kbuf[c * TOK:(c + 1) * TOK, cols] = jnp.dot(x, arena[width:2 * width, cols], preferred_element_type=jnp.float32).astype(jnp.bfloat16)
            vbuf[c * TOK:(c + 1) * TOK, cols] = jnp.dot(x, arena[2 * width:3 * width, cols], preferred_element_type=jnp.float32).astype(jnp.bfloat16)
            return 0
        with jax.named_scope('project'):
            lax.fori_loop(0, n_col, project, 0)
        hook(0)
        seen = (c + 1) * TOK
        q_at = lax.broadcasted_iota(jnp.int32, (TOK, seen), 0) + c * TOK
        k_at = lax.broadcasted_iota(jnp.int32, (TOK, seen), 1)
        causal = q_at >= k_at

        def head(h, _):
            cols = [pl.ds(pl.multiple_of((h * GROUP + u) * head_dim, head_dim), head_dim) for u in range(GROUP)]
            logits = [lax.dot_general(qbuf[:, at], kbuf[0:seen, at], (((1,), (1,)), ((), ())), preferred_element_type=jnp.float32) for at in cols]
            logits = [jnp.where(causal, s * (head_dim ** -0.5), -1e30) for s in logits]
            probs = [jnp.exp(s - jnp.max(s, axis=-1, keepdims=True)) for s in logits]
            sums = [jnp.sum(p, axis=-1, keepdims=True) for p in probs]
            mixed = [jnp.dot(p.astype(jnp.bfloat16), vbuf[0:seen, at], preferred_element_type=jnp.float32) for p, at in zip(probs, cols)]
            for at, m, t in zip(cols, mixed, sums):
                xbuf[:, at] = (m / t).astype(jnp.bfloat16)
            return 0
        with jax.named_scope('heads'):
            lax.fori_loop(0, heads // GROUP, head, 0)
        hook(1)

        def output(k, _):
            for u in range(2):
                n = c * n_out + 2 * k + u
                cols = pl.ds(pl.multiple_of((2 * k + u) * OUT, OUT), OUT)
                w_copy(n).wait()
                proj = jnp.dot(xbuf[...], wo_buf[n % WSLOT], preferred_element_type=jnp.float32).astype(jnp.bfloat16)
                zrecv[c, :, cols] = (zrecv[c, :, cols].astype(jnp.float32) + proj.astype(jnp.float32)).astype(jnp.bfloat16)

                @pl.when(n + WSLOT < n_tok * n_out)
                def _():
                    w_copy(n + WSLOT).start()
            return 0
        with jax.named_scope('output'):
            lax.fori_loop(0, n_out // 2, output, 0)
        pltpu.make_async_copy(zrecv.at[c], out_hbm.at[c], out_sem.at[c]).start()
        hook(2)

    with jax.named_scope('relay'):
        relay(0)
        finish(6)
        relay(1)
        relay(2)
    finish(7)
    plan = {(0, 0): (8,), (0, 2): (9,), (1, 0): (10,), (1, 2): (11, 12), (2, 0): (13,), (2, 2): (14, 15)}
    for c in range(n_tok):
        def hook(at, c=c):
            for j in plan.get((c, at), ()):
                with jax.named_scope('fin'):
                    finish(j)
        with jax.named_scope('attend'):
            attend(c, hook)

    def drain(i, _):
        y_copy(i).wait_send()
        z_copy(i).wait_send()
        return 0
    lax.fori_loop(0, n_piece, drain, 0)
    for d in range(n_col):
        d_copy(d).wait_send()
    for r in range(3):
        for k in range(3):
            t_copy(k, r).wait_send()
    for c in range(n_tok):
        pltpu.make_async_copy(zrecv.at[c], out_hbm.at[c], out_sem.at[c]).wait()


def run_stage(pp_size, expert_out, ids, slot, gate, resid, scale, wq, wk, wv, wo):
    experts, cap_all, width = expert_out.shape
    tokens = resid.shape[0]
    heads = wq.shape[1]
    slots = experts * cap_all // 4
    n_tok, n_col = tokens // TOK, width // COL
    n_piece = n_tok * n_col
    dma = pltpu.SemaphoreType.DMA
    anyspace = pl.BlockSpec(memory_space=pl.ANY)
    vmem = pl.BlockSpec(memory_space=pltpu.VMEM)
    f32, bf16 = jnp.float32, jnp.bfloat16
    return pl.pallas_call(
        functools.partial(stage_kernel, pp_size, heads),
        out_shape=jax.ShapeDtypeStruct((n_tok, TOK, width), bf16),
        in_specs=[anyspace, vmem, vmem, vmem, anyspace, vmem, anyspace, anyspace, anyspace, anyspace],
        out_specs=anyspace,
        scratch_shapes=[
            pltpu.VMEM((max(4 * slots, 3 * width), width), bf16),
            pltpu.VMEM((3, 8, tokens), jnp.int32), pltpu.VMEM((3, 8, tokens), jnp.int32), pltpu.VMEM((3, 8, tokens), f32),
            pltpu.VMEM((tokens, 64), f32),
            pltpu.VMEM((3 * TOK, slots), bf16), pltpu.VMEM((3 * TOK, slots), bf16),
            pltpu.VMEM((n_piece, TOK, COL), f32), pltpu.VMEM((n_piece, TOK, COL), f32), pltpu.VMEM((n_piece, TOK, COL), f32),
            pltpu.VMEM((n_col, TOK, COL), f32), pltpu.VMEM((n_col, TOK, COL), f32),
            pltpu.VMEM((n_piece, TOK, COL), bf16),
            pltpu.VMEM((n_tok, TOK, width), bf16),
            pltpu.VMEM((STAGED, BLK, heads, width // heads), bf16),
            pltpu.VMEM((WSLOT, width, OUT), bf16),
            pltpu.VMEM((TOK, width), bf16), pltpu.VMEM((tokens, width), bf16), pltpu.VMEM((tokens, width), bf16), pltpu.VMEM((TOK, width), bf16),
            dma((4,)), dma((n_piece,)), dma((3, 3)), dma((3, 3)), dma((n_col,)), dma((n_col,)),
            pltpu.SemaphoreType.REGULAR,
            dma((n_piece,)), dma((n_piece,)), dma((n_piece,)), dma((n_piece,)), dma((STAGED,)), dma((WSLOT,)), dma((n_tok,)),
        ],
        compiler_params=pltpu.CompilerParams(collective_id=0, has_side_effects=True, vmem_limit_bytes=67043328),
    )(expert_out, ids, slot, gate, resid, scale, wq, wk, wv, wo)


def solution(mesh):
    pp_size = mesh.shape['pp']
    token_spec = P(('data', 'pp'), 'ep', None, None)
    weight_spec = P('pp', None, None, None)

    def body(expert_out, expert_ids, slot_ids, gate_vals, residual, norm_scale, w_query, w_key, w_value, w_out):
        ids, slot, gate = (jnp.swapaxes(a[0, 0], 0, 1) for a in (expert_ids, slot_ids, gate_vals))
        width = expert_out.shape[-1]
        result = run_stage(pp_size, expert_out[0], ids, slot, gate, residual[0, 0], norm_scale, w_query[0], w_key[0], w_value[0], w_out[0].reshape(-1, width))
        return result.reshape(residual.shape)

    return jax.shard_map(body, mesh=mesh, in_specs=(token_spec, token_spec, token_spec, token_spec, token_spec, P('pp', None), weight_spec, weight_spec, weight_spec, weight_spec), out_specs=token_spec, check_vma=False)
```

time: 206 us -> 132 us (0.64)
  Pallas kernels: 201 us -> 128 us
    pallas_call x1, Pallas kernels: 201 us -> 128 us  [run_stage(): pl.pallas_call(functools.partial(stage_kernel, pp_size, heads), out_shape...]
where the time goes in v3:
time: 132 us; the launch traced here: 131 us
  Pallas kernels  128 us (97%)
  local copies, waits for them, and re-layouts  3.16 us (2%)
    pallas_call x1, Pallas kernels, run_stage(): pl.pallas_call(functools.partial(stage_kernel, pp_size, heads), out_shape...  128 us
    unnamed x1, local copies, waits for them, and re-layouts  3.16 us

profile of v3, /device:TPU:0, one launch (start us, length us, event | category | flops | bytes accessed | tf_op | source)
XLA Modules:
  0.0 131.3 jit_solution(14665050232510114319)
XLA Ops:
  0.0 128.2 %shard_map.100 = bf16[4,128,2048]{2,1,0:T(8,128)(2,1)} custom-call(bf16[16,320,2048]{2,1,0:T(8,128)(2,1)} %bitcast.16, s32[8,512]{1,0:T(8,128)} %bitcast.23, s32[8,512]{1,0:T(8,128)} %bitcast.24, f32[8,512]{1,0:T(8,128)} %bitcast.25, bf16[512,2048]{1,0:T(8,128)(2,1)} %bitcast.22, f32[1,2048]{1,0:T(1,128)} %scale_in.1, bf16[2048,16,128]{2,1,0:T(8,128)(2,1)} %bitcast.18, ...), custom_call_target="tpu_custom_call" | custom-call | tf_op jit(solution)/shard_map/pallas_call | solution.py:370
  128.2 3.2 %copy.12 = bf16[1,1,512,2048]{3,2,1,0:T(8,128)(2,1)} copy(bf16[1,1,512,2048]{3,2,1,0:T(8,128)(2,1)} %bitcast.17) | data formatting | bytes 4194304

commit v4 on v3

--- a/solution.py
+++ b/solution.py
@@ -17,11 +17,12 @@
 OUT = 256
 WSLOT = 6
 GROUP = 8
+PARTS = 4
 
 
 def stage_kernel(pp_size, heads, o_hbm, ids_in, slot_in, gate_in, h_hbm, scale_in, wq_hbm, wk_hbm, wv_hbm, wo_hbm, out_hbm,
                  arena, tids, tslot, tgate, tblt, gate_a, gate_b, ysend, acc, yrecv, dsend, drecv, hz, zrecv, stage_buf, wo_buf, qbuf, kbuf, vbuf, xbuf,
-                 o_sem, h_sem, t_ssem, t_rsem, d_ssem, d_rsem, credit, y_ssem, y_rsem, z_ssem, z_rsem, s_sem, w_sem, out_sem):
+                 o_sem, h_sem, t_ssem, t_rsem, d_ssem, d_rsem, credit, y_ssem, y_rsem, z_ssem, z_rsem, yp_ssem, yp_rsem, zp_ssem, zp_rsem, s_sem, w_sem, out_sem):
     experts, cap_all, width = o_hbm.shape
     cap = cap_all // 4
     slots = experts * cap
@@ -76,6 +77,19 @@
         return pltpu.make_async_remote_copy(src_ref=hz.at[i], dst_ref=zrecv.at[c, :, pl.ds(pl.multiple_of(d * COL, COL), COL)],
                                             send_sem=z_ssem.at[i], recv_sem=z_rsem.at[i], device_id={'pp': nxt}, device_id_type=MESH)
 
+    last = n_piece - 1
+    thin = TOK // PARTS
+
+    def y_part(k):
+        rows = pl.ds(k * thin, thin)
+        return pltpu.make_async_remote_copy(src_ref=ysend.at[last, rows], dst_ref=yrecv.at[last, rows], send_sem=yp_ssem.at[k],
+                                            recv_sem=yp_rsem.at[k], device_id={'ep': peer}, device_id_type=MESH)
+
+    def z_part(k):
+        rows = pl.ds(k * thin, thin)
+        return pltpu.make_async_remote_copy(src_ref=hz.at[last, rows], dst_ref=zrecv.at[n_tok - 1, rows, pl.ds(width - COL, COL)],
+                                            send_sem=zp_ssem.at[k], recv_sem=zp_rsem.at[k], device_id={'pp': nxt}, device_id_type=MESH)
+
     raw = (wq_hbm, wk_hbm, wv_hbm)
 
     n_blk = width // BLK
@@ -124,19 +138,15 @@
     halves = width // WIDE
     per = WIDE // COL
 
-    def phase(c, r, ahead, before, use):
-        def half(h, _):
-            before(h)
-            w = arena[r * slots:(r + 1) * slots, pl.ds(pl.multiple_of(h * WIDE, WIDE), WIDE)]
-            p = jnp.dot(gates[r % 2][...], w, preferred_element_type=jnp.float32)
-            total = p[:TOK] + p[TOK:2 * TOK] + p[2 * TOK:]
-            if ahead is not None:
-                for q in range(groups // halves):
-                    build(*ahead, h * (groups // halves) + q)
-            for u in range(per):
-                use(h * per + u, total[:, u * COL:(u + 1) * COL])
-            return 0
-        lax.fori_loop(0, halves, half, 0)
+    def dot_role(r, h):
+        w = arena[r * slots:(r + 1) * slots, h * WIDE:(h + 1) * WIDE]
+        p = jnp.dot(gates[r % 2][...], w, preferred_element_type=jnp.float32)
+        total = p[:TOK] + p[TOK:2 * TOK] + p[2 * TOK:]
+        return [(h * per + u, total[:, u * COL:(u + 1) * COL]) for u in range(per)]
+
+    def build_now(c, r):
+        for q in range(groups):
+            build(c, r, q)
 
     def give():
         pl.semaphore_signal(credit, inc=1, device_id={'ep': partner}, device_id_type=MESH)
@@ -144,38 +154,19 @@
     def hold(d):
         d_copy(d).wait_send()
         pl.semaphore_wait(credit, 1)
-
-    def send_core(d, value):
-        dsend[d] = value
-        d_copy(d).start()
-
-    def self_role(c, ahead):
-        def before(h):
-            for u in range(per):
-                h_copy(c * n_col + h * per + u).wait()
-
-        def use(d, value):
-            i = c * n_col + d
-            acc[i] = value + hz[i].astype(jnp.float32)
-        phase(c, 3, ahead, before, use)
-
-    def take_local(c):
-        def one(d, _):
-            d_copy(d).wait_recv()
-            acc[c * n_col + d] += drecv[d]
-
-            @pl.when(c < n_tok - 1)
-            def _():
-                give()
-            return 0
-        lax.fori_loop(0, n_col, one, 0)
 
     def finish(j):
         y_copy(j).wait_recv()
         hz[j] = (acc[j] + yrecv[j]).astype(jnp.bfloat16)
         z_copy(j).start()
 
-    o_start(3)
+    def finish_last():
+        for k in range(PARTS):
+            rows = pl.ds(k * thin, thin)
+            y_part(k).wait_recv()
+            hz[last, rows] = (acc[last, rows] + yrecv[last, rows]).astype(jnp.bfloat16)
+            z_part(k).start()
+
     o_start(0)
     barrier = pltpu.get_barrier_semaphore()
     for dev in (partner, peer, diag):
@@ -184,22 +175,20 @@
         pl.semaphore_signal(barrier, inc=1, device_id={'pp': dev}, device_id_type=MESH)
     for i in range(n_col):
         h_copy(i).start()
-    keyed(3, ids_in[...], slot_in[...], gate_in[...])
+    o_start(1)
     pl.semaphore_wait(barrier, 5)
     for r in range(3):
         for k in range(3):
             t_copy(k, r).start()
-    build_all(0, 3)
-    o_start(1)
+    keyed(3, ids_in[...], slot_in[...], gate_in[...])
     o_start(2)
-    o_wait(3)
-    self_role(0, None)
+    o_start(3)
     for r in range(3):
         for k in range(3):
             t_copy(k, r).wait_recv()
         keyed(r, tids[r], tslot[r], tgate[r])
     build_all(0, 0)
-    for r in range(3):
+    for r in range(4):
         o_wait(r)
 
     def rest_h(i, _):
@@ -212,33 +201,61 @@
         w_copy(n).start()
 
     def chunk(c, _):
-        def hold0(h):
+        for h in range(halves):
             @pl.when(c > 0)
             def _():
                 for u in range(per):
                     hold(h * per + u)
-        phase(c, 0, (c, 1), hold0, send_core)
-
-        def got(h):
+            for d, value in dot_role(0, h):
+                dsend[d] = value
+            if h == 0:
+                build_now(c, 1)
             for u in range(per):
-                d_copy(h * per + u).wait_recv()
-
-        def merge(d, value):
-            i = c * n_col + d
-            ysend[i] = value + drecv[d]
-            give()
-            y_copy(i).start()
-        phase(c, 1, (c, 2), got, merge)
-
-        def hold2(h):
+                d_copy(h * per + u).start()
+            for d, value in dot_role(1, h):
+                ysend[c * n_col + d] = value
+            if h == halves - 1:
+                build_now(c, 2)
+            for u in range(per):
+                d = h * per + u
+                i = c * n_col + d
+                d_copy(d).wait_recv()
+                ysend[i] += drecv[d]
+                give()
+                if d < n_col - 1:
+                    y_copy(i).start()
+                else:
+                    @pl.when(c < n_tok - 1)
+                    def _():
+                        y_copy(i).start()
+
+                    @pl.when(c == n_tok - 1)
+                    def _():
+                        for k in range(PARTS):
+                            y_part(k).start()
+        for h in range(halves):
             for u in range(per):
                 hold(h * per + u)
-        phase(c, 2, (lax.rem(c + 1, n_tok), 3), hold2, send_core)
-
-        @pl.when(c < n_tok - 1)
-        def _():
-            self_role(c + 1, (c + 1, 0))
-        take_local(c)
+            for d, value in dot_role(2, h):
+                dsend[d] = value
+            if h == 0:
+                build_now(c, 3)
+            for u in range(per):
+                d_copy(h * per + u).start()
+                h_copy(c * n_col + h * per + u).wait()
+            for d, value in dot_role(3, h):
+                i = c * n_col + d
+                acc[i] = value + hz[i].astype(jnp.float32)
+            if h == halves - 1:
+                build_now(lax.rem(c + 1, n_tok), 0)
+            for u in range(per):
+                d = h * per + u
+                d_copy(d).wait_recv()
+                acc[c * n_col + d] += drecv[d]
+
+                @pl.when(c < n_tok - 1)
+                def _():
+                    give()
 
         @pl.when(c > 0)
         def _():
@@ -270,26 +287,27 @@
     def attend(c, hook):
         with jax.named_scope('zwait'):
             for d in range(n_col):
-                z_copy(c * n_col + d).wait_recv()
+                if c * n_col + d < last:
+                    z_copy(c * n_col + d).wait_recv()
+                else:
+                    for k in range(PARTS):
+                        z_part(k).wait_recv()
         scale = scale_in[...]
-
-        def norm(k, _):
-            rows = pl.ds(pl.multiple_of(k * 16, 16), 16)
+        for k in range(TOK // 16):
+            rows = slice(k * 16, (k + 1) * 16)
             x = zrecv[c, rows, :].astype(jnp.float32)
             inv = lax.rsqrt(jnp.mean(x * x, axis=-1, keepdims=True) + NORM_EPS)
             xbuf[rows, :] = (x * inv * scale).astype(jnp.bfloat16)
-            return 0
-        lax.fori_loop(0, TOK // 16, norm, 0)
 
         def project(n, _):
-            cols = pl.ds(pl.multiple_of(n * COL, COL), COL)
+            cols = pl.ds(pl.multiple_of(n * WIDE, WIDE), WIDE)
             x = xbuf[...]
             qbuf[:, cols] = jnp.dot(x, arena[0:width, cols], preferred_element_type=jnp.float32).astype(jnp.bfloat16)
             kbuf[c * TOK:(c + 1) * TOK, cols] = jnp.dot(x, arena[width:2 * width, cols], preferred_element_type=jnp.float32).astype(jnp.bfloat16)
             vbuf[c * TOK:(c + 1) * TOK, cols] = jnp.dot(x, arena[2 * width:3 * width, cols], preferred_element_type=jnp.float32).astype(jnp.bfloat16)
             return 0
         with jax.named_scope('project'):
-            lax.fori_loop(0, n_col, project, 0)
+            lax.fori_loop(0, halves, project, 0)
         hook(0)
         seen = (c + 1) * TOK
         q_at = lax.broadcasted_iota(jnp.int32, (TOK, seen), 0) + c * TOK
@@ -311,16 +329,18 @@
         hook(1)
 
         def output(k, _):
-            for u in range(2):
-                n = c * n_out + 2 * k + u
-                cols = pl.ds(pl.multiple_of((2 * k + u) * OUT, OUT), OUT)
-                w_copy(n).wait()
-                proj = jnp.dot(xbuf[...], wo_buf[n % WSLOT], preferred_element_type=jnp.float32).astype(jnp.bfloat16)
-                zrecv[c, :, cols] = (zrecv[c, :, cols].astype(jnp.float32) + proj.astype(jnp.float32)).astype(jnp.bfloat16)
-
-                @pl.when(n + WSLOT < n_tok * n_out)
-                def _():
-                    w_copy(n + WSLOT).start()
+            n = c * n_out + 2 * k
+            cols = pl.ds(pl.multiple_of(2 * k * OUT, 2 * OUT), 2 * OUT)
+            w_copy(n).wait()
+            w_copy(n + 1).wait()
+            w = jnp.concatenate([wo_buf[n % WSLOT], wo_buf[(n + 1) % WSLOT]], axis=1)
+            proj = jnp.dot(xbuf[...], w, preferred_element_type=jnp.float32).astype(jnp.bfloat16)
+            zrecv[c, :, cols] = (zrecv[c, :, cols].astype(jnp.float32) + proj.astype(jnp.float32)).astype(jnp.bfloat16)
+
+            @pl.when(n + WSLOT < n_tok * n_out)
+            def _():
+                w_copy(n + WSLOT).start()
+                w_copy(n + 1 + WSLOT).start()
             return 0
         with jax.named_scope('output'):
             lax.fori_loop(0, n_out // 2, output, 0)
@@ -338,7 +358,10 @@
         def hook(at, c=c):
             for j in plan.get((c, at), ()):
                 with jax.named_scope('fin'):
-                    finish(j)
+                    if j == last:
+                        finish_last()
+                    else:
+                        finish(j)
         with jax.named_scope('attend'):
             attend(c, hook)
 
@@ -346,7 +369,10 @@
         y_copy(i).wait_send()
         z_copy(i).wait_send()
         return 0
-    lax.fori_loop(0, n_piece, drain, 0)
+    lax.fori_loop(0, last, drain, 0)
+    for k in range(PARTS):
+        y_part(k).wait_send()
+        z_part(k).wait_send()
     for d in range(n_col):
         d_copy(d).wait_send()
     for r in range(3):
@@ -386,7 +412,7 @@
             pltpu.VMEM((TOK, width), bf16), pltpu.VMEM((tokens, width), bf16), pltpu.VMEM((tokens, width), bf16), pltpu.VMEM((TOK, width), bf16),
             dma((4,)), dma((n_piece,)), dma((3, 3)), dma((3, 3)), dma((n_col,)), dma((n_col,)),
             pltpu.SemaphoreType.REGULAR,
-            dma((n_piece,)), dma((n_piece,)), dma((n_piece,)), dma((n_piece,)), dma((STAGED,)), dma((WSLOT,)), dma((n_tok,)),
+            dma((n_piece,)), dma((n_piece,)), dma((n_piece,)), dma((n_piece,)), dma((PARTS,)), dma((PARTS,)), dma((PARTS,)), dma((PARTS,)), dma((STAGED,)), dma((WSLOT,)), dma((n_tok,)),
         ],
         compiler_params=pltpu.CompilerParams(collective_id=0, has_side_effects=True, vmem_limit_bytes=67043328),
     )(expert_out, ids, slot, gate, resid, scale, wq, wk, wv, wo)

time: 132 us -> 125 us (0.947)
  Pallas kernels: 128 us -> 121 us
    pallas_call x1, Pallas kernels: 128 us -> 121 us  [run_stage(): pl.pallas_call(functools.partial(stage_kernel, pp_size, heads), out_shape...]
where the time goes in v4:
time: 125 us; the launch traced here: 124 us
  Pallas kernels  121 us (97%)
  local copies, waits for them, and re-layouts  3.16 us (3%)
    pallas_call x1, Pallas kernels, run_stage(): pl.pallas_call(functools.partial(stage_kernel, pp_size, heads), out_shape...  121 us
    unnamed x1, local copies, waits for them, and re-layouts  3.16 us

profile of v4, /device:TPU:0, one launch (start us, length us, event | category | flops | bytes accessed | tf_op | source)
XLA Modules:
  0.0 124.4 jit_solution(10835680157550742139)
XLA Ops:
  0.0 121.2 %shard_map.100 = bf16[4,128,2048]{2,1,0:T(8,128)(2,1)} custom-call(bf16[16,320,2048]{2,1,0:T(8,128)(2,1)} %bitcast.16, s32[8,512]{1,0:T(8,128)} %bitcast.23, s32[8,512]{1,0:T(8,128)} %bitcast.24, f32[8,512]{1,0:T(8,128)} %bitcast.25, bf16[512,2048]{1,0:T(8,128)(2,1)} %bitcast.22, f32[1,2048]{1,0:T(1,128)} %scale_in.1, bf16[2048,16,128]{2,1,0:T(8,128)(2,1)} %bitcast.18, ...), custom_call_target="tpu_custom_call" | custom-call | tf_op jit(solution)/shard_map/pallas_call | solution.py:396
  121.3 3.2 %copy.12 = bf16[1,1,512,2048]{3,2,1,0:T(8,128)(2,1)} copy(bf16[1,1,512,2048]{3,2,1,0:T(8,128)(2,1)} %bitcast.17) | data formatting | bytes 4194304

commit v5 on v4

--- a/solution.py
+++ b/solution.py
@@ -13,16 +13,13 @@
 COL = 512
 WIDE = 1024
 BLK = 128
-STAGED = 6
-OUT = 256
-WSLOT = 6
-GROUP = 8
+GROUP = 16
 PARTS = 4
 
 
 def stage_kernel(pp_size, heads, o_hbm, ids_in, slot_in, gate_in, h_hbm, scale_in, wq_hbm, wk_hbm, wv_hbm, wo_hbm, out_hbm,
-                 arena, tids, tslot, tgate, tblt, gate_a, gate_b, ysend, acc, yrecv, dsend, drecv, hz, zrecv, stage_buf, wo_buf, qbuf, kbuf, vbuf, xbuf,
-                 o_sem, h_sem, t_ssem, t_rsem, d_ssem, d_rsem, credit, y_ssem, y_rsem, z_ssem, z_rsem, yp_ssem, yp_rsem, zp_ssem, zp_rsem, s_sem, w_sem, out_sem):
+                 arena, mine, theirs, tblt, gate_a, gate_b, ysend, acc, yrecv, dsend, drecv, hz, zrecv, panel, qbuf, kbuf, vbuf, xbuf,
+                 o_sem, h_sem, t_ssem, t_rsem, d_ssem, d_rsem, credit, y_ssem, y_rsem, z_ssem, z_rsem, yp_ssem, yp_rsem, zp_ssem, zp_rsem, s_sem, out_sem):
     experts, cap_all, width = o_hbm.shape
     cap = cap_all // 4
     slots = experts * cap
@@ -30,7 +27,6 @@
     head_dim = width // heads
     n_tok, n_col = tokens // TOK, width // COL
     n_piece = n_tok * n_col
-    n_out = width // OUT
     gates = (gate_b, gate_a)
     me = lax.axis_index('ep')
     core = lax.rem(me, 2)
@@ -58,11 +54,9 @@
         c, d = i // n_col, i % n_col
         return pltpu.make_async_copy(h_hbm.at[pl.ds(c * TOK, TOK), pl.ds(d * COL, COL)], hz.at[i], h_sem.at[i])
 
-    tables = ((ids_in, tids), (slot_in, tslot), (gate_in, tgate))
-
-    def t_copy(k, r):
-        return pltpu.make_async_remote_copy(src_ref=tables[k][0], dst_ref=tables[k][1].at[r], send_sem=t_ssem.at[k, r],
-                                            recv_sem=t_rsem.at[k, r], device_id={'ep': owners[r]}, device_id_type=MESH)
+    def t_copy(r):
+        return pltpu.make_async_remote_copy(src_ref=mine, dst_ref=theirs.at[r], send_sem=t_ssem.at[r], recv_sem=t_rsem.at[r],
+                                            device_id={'ep': owners[r]}, device_id_type=MESH)
 
     def d_copy(d):
         return pltpu.make_async_remote_copy(src_ref=dsend.at[d], dst_ref=drecv.at[d], send_sem=d_ssem.at[d],
@@ -93,23 +87,19 @@
     raw = (wq_hbm, wk_hbm, wv_hbm)
 
     n_blk = width // BLK
-
-    def s_copy(w, b, at):
-        return pltpu.make_async_copy(raw[w].at[pl.ds(b * BLK, BLK)], stage_buf.at[at], s_sem.at[at])
-
-    def s_start(m):
-        for w in range(3):
-            @pl.when(m // n_blk == w)
-            def _():
-                s_copy(w, m % n_blk, m % STAGED).start()
-
-    def w_copy(n):
-        at = n % WSLOT
-        return pltpu.make_async_copy(wo_hbm.at[:, pl.ds(pl.multiple_of(n % n_out * OUT, OUT), OUT)], wo_buf.at[at], w_sem.at[at])
-
-    def keyed(r, ids, slot, gate):
-        key = jnp.where(slot >= 0, (ids - me * experts) * cap + (slot - owners[r] * cap), -1).astype(jnp.float32)
-        tblt[:, r * 16:(r + 1) * 16] = jnp.transpose(jnp.concatenate([key, gate], axis=0))
+    rows_blk = BLK * heads
+
+    def s_copy(w, b):
+        return pltpu.make_async_copy(raw[w].at[pl.ds(b * rows_blk, rows_blk)], panel.at[b], s_sem.at[b])
+
+    def w_copy(q):
+        return pltpu.make_async_copy(wo_hbm.at[:, pl.ds(q * head_dim, head_dim)], panel.at[q], s_sem.at[q])
+
+    lane_row = lax.broadcasted_iota(jnp.int32, (16, tokens), 0)
+
+    def keyed(r, table):
+        shift = jnp.where(lane_row < 8, me * slots, 0).astype(jnp.float32)
+        tblt[:, r * 16:(r + 1) * 16] = jnp.transpose(table - shift)
 
     groups = TOK // 16
 
@@ -129,20 +119,13 @@
         dst[pl.ds(at + TOK, 16), :] = g2
         dst[pl.ds(at + 2 * TOK, 16), :] = g3
 
-    def build_all(c, r):
-        def one(q, _):
-            build(c, r, q)
-            return 0
-        lax.fori_loop(0, groups, one, 0)
-
     halves = width // WIDE
-    per = WIDE // COL
-
-    def dot_role(r, h):
-        w = arena[r * slots:(r + 1) * slots, h * WIDE:(h + 1) * WIDE]
+
+    def dot_role(r, h, per):
+        w = arena[r * slots:(r + 1) * slots, h * COL:(h + per) * COL]
         p = jnp.dot(gates[r % 2][...], w, preferred_element_type=jnp.float32)
         total = p[:TOK] + p[TOK:2 * TOK] + p[2 * TOK:]
-        return [(h * per + u, total[:, u * COL:(u + 1) * COL]) for u in range(per)]
+        return [(h + u, total[:, u * COL:(u + 1) * COL]) for u in range(per)]
 
     def build_now(c, r):
         for q in range(groups):
@@ -173,89 +156,114 @@
         pl.semaphore_signal(barrier, inc=1, device_id={'ep': dev}, device_id_type=MESH)
     for dev in (nxt, prv):
         pl.semaphore_signal(barrier, inc=1, device_id={'pp': dev}, device_id_type=MESH)
+    slot = slot_in[...]
+    mine[0:8] = jnp.where(slot >= 0, ids_in[...] * cap + (slot - me * cap), -1).astype(jnp.float32)
+    mine[8:16] = gate_in[...]
+    pl.semaphore_wait(barrier, 5)
+    for r in range(3):
+        t_copy(r).start()
+    o_start(1)
+    keyed(3, mine[...])
     for i in range(n_col):
         h_copy(i).start()
-    o_start(1)
-    pl.semaphore_wait(barrier, 5)
     for r in range(3):
-        for k in range(3):
-            t_copy(k, r).start()
-    keyed(3, ids_in[...], slot_in[...], gate_in[...])
+        t_copy(r).wait_recv()
+        keyed(r, theirs[r])
+        if r == 0:
+            build_now(0, 0)
     o_start(2)
     o_start(3)
-    for r in range(3):
-        for k in range(3):
-            t_copy(k, r).wait_recv()
-        keyed(r, tids[r], tslot[r], tgate[r])
-    build_all(0, 0)
-    for r in range(4):
-        o_wait(r)
 
     def rest_h(i, _):
         h_copy(i).start()
         return 0
     lax.fori_loop(n_col, n_piece, rest_h, 0)
-    for m in range(STAGED - 1):
-        s_copy(0, m, m).start()
-    for n in range(WSLOT):
-        w_copy(n).start()
+
+    def at_first(c, r):
+        @pl.when(c == 0)
+        def _():
+            o_wait(r)
 
     def chunk(c, _):
-        for h in range(halves):
-            @pl.when(c > 0)
-            def _():
-                for u in range(per):
-                    hold(h * per + u)
-            for d, value in dot_role(0, h):
+        @pl.when(c == 1)
+        def _():
+            for q in range(n_blk):
+                s_copy(0, q).start()
+
+        def fill(d):
+            i = c * n_col + d
+            d_copy(d).wait_recv()
+            ysend[i] += drecv[d]
+            give()
+            if d < n_col - 1:
+                y_copy(i).start()
+            else:
+                @pl.when(c < n_tok - 1)
+                def _():
+                    y_copy(i).start()
+
+                @pl.when(c == n_tok - 1)
+                def _():
+                    for k in range(PARTS):
+                        y_part(k).start()
+
+        def out_role(r, h, per, ahead=None):
+            for d in range(h, h + per):
+                if r == 0:
+                    @pl.when(c > 0)
+                    def _():
+                        hold(d)
+                else:
+                    hold(d)
+            if h == 0:
+                at_first(c, r)
+            for d, value in dot_role(r, h, per):
                 dsend[d] = value
+            if ahead is not None:
+                build_now(*ahead)
+            for d in range(h, h + per):
+                d_copy(d).start()
+
+        def near_role(h, per, ahead=None):
             if h == 0:
-                build_now(c, 1)
-            for u in range(per):
-                d_copy(h * per + u).start()
-            for d, value in dot_role(1, h):
+                at_first(c, 1)
+            for d, value in dot_role(1, h, per):
                 ysend[c * n_col + d] = value
-            if h == halves - 1:
-                build_now(c, 2)
-            for u in range(per):
-                d = h * per + u
-                i = c * n_col + d
-                d_copy(d).wait_recv()
-                ysend[i] += drecv[d]
-                give()
-                if d < n_col - 1:
-                    y_copy(i).start()
-                else:
-                    @pl.when(c < n_tok - 1)
-                    def _():
-                        y_copy(i).start()
-
-                    @pl.when(c == n_tok - 1)
-                    def _():
-                        for k in range(PARTS):
-                            y_part(k).start()
-        for h in range(halves):
-            for u in range(per):
-                hold(h * per + u)
-            for d, value in dot_role(2, h):
-                dsend[d] = value
+            if ahead is not None:
+                build_now(*ahead)
+            for d in range(h, h + per):
+                fill(d)
+
+        def own_role(h, per, ahead=None):
+            for d in range(h, h + per):
+                h_copy(c * n_col + d).wait()
             if h == 0:
-                build_now(c, 3)
-            for u in range(per):
-                d_copy(h * per + u).start()
-                h_copy(c * n_col + h * per + u).wait()
-            for d, value in dot_role(3, h):
+                at_first(c, 3)
+            for d, value in dot_role(3, h, per):
                 i = c * n_col + d
                 acc[i] = value + hz[i].astype(jnp.float32)
-            if h == halves - 1:
-                build_now(lax.rem(c + 1, n_tok), 0)
-            for u in range(per):
-                d = h * per + u
+            if ahead is not None:
+                build_now(*ahead)
+            for d in range(h, h + per):
                 d_copy(d).wait_recv()
                 acc[c * n_col + d] += drecv[d]
 
                 @pl.when(c < n_tok - 1)
                 def _():
                     give()
+
+        half = n_col // 2
+        out_role(0, 0, 1, (c, 1))
+        for d in range(1, half):
+            out_role(0, d, 1)
+        for d in range(half):
+            near_role(d, 1)
+        out_role(0, half, half)
+        near_role(half, half, (c, 2))
+        out_role(2, 0, half, (c, 3))
+        out_role(2, half, half)
+        own_role(0, half)
+        own_role(half, half, (lax.rem(c + 1, n_tok), 0))
 
         @pl.when(c > 0)
         def _():
@@ -268,21 +276,20 @@
 
     def relay(w):
         def block(b, _):
-            m = w * n_blk + b
-            at = m % STAGED
-            s_copy(w, b, at).wait()
-
-            @pl.when(m + STAGED - 1 < 3 * n_blk)
-            def _():
-                s_start(m + STAGED - 1)
-
-            def sub(k, _):
-                rows = pl.multiple_of(k * 64, 64)
-                arena[pl.ds(pl.multiple_of(w * width + b * BLK + rows, 64), 64), :] = stage_buf[at, pl.ds(rows, 64)].reshape(64, width)
-                return 0
-            lax.fori_loop(0, BLK // 64, sub, 0)
+            s_copy(w, b).wait()
+            for k in range(BLK // 64):
+                rows = panel[b, k * 64 * heads:(k + 1) * 64 * heads, :].reshape(64, heads, head_dim).reshape(64, width)
+                arena[pl.ds(pl.multiple_of(w * width + b * BLK + k * 64, 64), 64), :] = rows
+            if w < 2:
+                s_copy(w + 1, b).start()
+            else:
+                w_copy(b).start()
             return 0
         lax.fori_loop(0, n_blk, block, 0)
+
+    def out_copy(c, k):
+        cols = pl.ds(k * WIDE, WIDE)
+        return pltpu.make_async_copy(zrecv.at[c, :, cols], out_hbm.at[c, :, cols], out_sem.at[c, k])
 
     def attend(c, hook):
         with jax.named_scope('zwait'):
@@ -328,32 +335,26 @@
             lax.fori_loop(0, heads // GROUP, head, 0)
         hook(1)
 
-        def output(k, _):
-            n = c * n_out + 2 * k
-            cols = pl.ds(pl.multiple_of(2 * k * OUT, 2 * OUT), 2 * OUT)
-            w_copy(n).wait()
-            w_copy(n + 1).wait()
-            w = jnp.concatenate([wo_buf[n % WSLOT], wo_buf[(n + 1) % WSLOT]], axis=1)
-            proj = jnp.dot(xbuf[...], w, preferred_element_type=jnp.float32).astype(jnp.bfloat16)
-            zrecv[c, :, cols] = (zrecv[c, :, cols].astype(jnp.float32) + proj.astype(jnp.float32)).astype(jnp.bfloat16)
-
-            @pl.when(n + WSLOT < n_tok * n_out)
-            def _():
-                w_copy(n + WSLOT).start()
-                w_copy(n + 1 + WSLOT).start()
-            return 0
+        if c == 0:
+            for q in range(heads):
+                w_copy(q).wait()
         with jax.named_scope('output'):
-            lax.fori_loop(0, n_out // 2, output, 0)
-        pltpu.make_async_copy(zrecv.at[c], out_hbm.at[c], out_sem.at[c]).start()
+            for k in range(halves):
+                cols = slice(k * WIDE, (k + 1) * WIDE)
+                w = jnp.concatenate([panel[q] for q in range(k * WIDE // head_dim, (k + 1) * WIDE // head_dim)], axis=1)
+                proj = jnp.dot(xbuf[...], w, preferred_element_type=jnp.float32).astype(jnp.bfloat16)
+                zrecv[c, :, cols] = (zrecv[c, :, cols].astype(jnp.float32) + proj.astype(jnp.float32)).astype(jnp.bfloat16)
+                out_copy(c, k).start()
         hook(2)
 
+    finish(6)
     with jax.named_scope('relay'):
         relay(0)
-        finish(6)
         relay(1)
+        finish(7)
         relay(2)
-    finish(7)
-    plan = {(0, 0): (8,), (0, 2): (9,), (1, 0): (10,), (1, 2): (11, 12), (2, 0): (13,), (2, 2): (14, 15)}
+    finish(8)
+    plan = {(0, 2): (9,), (1, 2): (10, 11), (2, 0): (12,), (2, 1): (13,), (2, 2): (14, 15)}
     for c in range(n_tok):
         def hook(at, c=c):
             for j in plan.get((c, at), ()):
@@ -376,16 +377,33 @@
     for d in range(n_col):
         d_copy(d).wait_send()
     for r in range(3):
-        for k in range(3):
-            t_copy(k, r).wait_send()
+        t_copy(r).wait_send()
     for c in range(n_tok):
-        pltpu.make_async_copy(zrecv.at[c], out_hbm.at[c], out_sem.at[c]).wait()
-
-
-def run_stage(pp_size, expert_out, ids, slot, gate, resid, scale, wq, wk, wv, wo):
+        for k in range(halves):
+            out_copy(c, k).wait()
+
+
+def copy_kernel(src, dst, hold, in_sem, out_sem):
+    steps = src.shape[0]
+    for c in range(steps):
+        pltpu.make_async_copy(src.at[c], hold.at[c], in_sem.at[c]).start()
+    for c in range(steps):
+        pltpu.make_async_copy(src.at[c], hold.at[c], in_sem.at[c]).wait()
+        pltpu.make_async_copy(hold.at[c], dst.at[c], out_sem.at[c]).start()
+    for c in range(steps):
+        pltpu.make_async_copy(hold.at[c], dst.at[c], out_sem.at[c]).wait()
+
+
+def settle(x):
+    anyspace = pl.BlockSpec(memory_space=pl.ANY)
+    dma = pltpu.SemaphoreType.DMA
+    return pl.pallas_call(copy_kernel, out_shape=jax.ShapeDtypeStruct(x.shape, x.dtype), in_specs=[anyspace], out_specs=anyspace,
+                          scratch_shapes=[pltpu.VMEM(x.shape, x.dtype), dma((x.shape[0],)), dma((x.shape[0],))])(x)
+
+
+def run_stage(pp_size, heads, expert_out, ids, slot, gate, resid, scale, wq, wk, wv, wo):
     experts, cap_all, width = expert_out.shape
     tokens = resid.shape[0]
-    heads = wq.shape[1]
     slots = experts * cap_all // 4
     n_tok, n_col = tokens // TOK, width // COL
     n_piece = n_tok * n_col
@@ -400,19 +418,18 @@
         out_specs=anyspace,
         scratch_shapes=[
             pltpu.VMEM((max(4 * slots, 3 * width), width), bf16),
-            pltpu.VMEM((3, 8, tokens), jnp.int32), pltpu.VMEM((3, 8, tokens), jnp.int32), pltpu.VMEM((3, 8, tokens), f32),
+            pltpu.VMEM((16, tokens), f32), pltpu.VMEM((3, 16, tokens), f32),
             pltpu.VMEM((tokens, 64), f32),
             pltpu.VMEM((3 * TOK, slots), bf16), pltpu.VMEM((3 * TOK, slots), bf16),
             pltpu.VMEM((n_piece, TOK, COL), f32), pltpu.VMEM((n_piece, TOK, COL), f32), pltpu.VMEM((n_piece, TOK, COL), f32),
             pltpu.VMEM((n_col, TOK, COL), f32), pltpu.VMEM((n_col, TOK, COL), f32),
             pltpu.VMEM((n_piece, TOK, COL), bf16),
             pltpu.VMEM((n_tok, TOK, width), bf16),
-            pltpu.VMEM((STAGED, BLK, heads, width // heads), bf16),
-            pltpu.VMEM((WSLOT, width, OUT), bf16),
+            pltpu.VMEM((width // BLK, width, width // heads), bf16),
             pltpu.VMEM((TOK, width), bf16), pltpu.VMEM((tokens, width), bf16), pltpu.VMEM((tokens, width), bf16), pltpu.VMEM((TOK, width), bf16),
-            dma((4,)), dma((n_piece,)), dma((3, 3)), dma((3, 3)), dma((n_col,)), dma((n_col,)),
+            dma((4,)), dma((n_piece,)), dma((3,)), dma((3,)), dma((n_col,)), dma((n_col,)),
             pltpu.SemaphoreType.REGULAR,
-            dma((n_piece,)), dma((n_piece,)), dma((n_piece,)), dma((n_piece,)), dma((PARTS,)), dma((PARTS,)), dma((PARTS,)), dma((PARTS,)), dma((STAGED,)), dma((WSLOT,)), dma((n_tok,)),
+            dma((n_piece,)), dma((n_piece,)), dma((n_piece,)), dma((n_piece,)), dma((PARTS,)), dma((PARTS,)), dma((PARTS,)), dma((PARTS,)), dma((width // BLK,)), dma((n_tok, width // WIDE)),
         ],
         compiler_params=pltpu.CompilerParams(collective_id=0, has_side_effects=True, vmem_limit_bytes=67043328),
     )(expert_out, ids, slot, gate, resid, scale, wq, wk, wv, wo)
@@ -425,8 +442,8 @@
 
     def body(expert_out, expert_ids, slot_ids, gate_vals, residual, norm_scale, w_query, w_key, w_value, w_out):
         ids, slot, gate = (jnp.swapaxes(a[0, 0], 0, 1) for a in (expert_ids, slot_ids, gate_vals))
-        width = expert_out.shape[-1]
-        result = run_stage(pp_size, expert_out[0], ids, slot, gate, residual[0, 0], norm_scale, w_query[0], w_key[0], w_value[0], w_out[0].reshape(-1, width))
-        return result.reshape(residual.shape)
+        result = run_stage(pp_size, w_query.shape[2], expert_out[0], ids, slot, gate, residual[0, 0], norm_scale,
+                           *(w[0].reshape(-1, w.shape[-1]) for w in (w_query, w_key, w_value, w_out)))
+        return settle(result).reshape(residual.shape)
 
     return jax.shard_map(body, mesh=mesh, in_specs=(token_spec, token_spec, token_spec, token_spec, token_spec, P('pp', None), weight_spec, weight_spec, weight_spec, weight_spec), out_specs=token_spec, check_vma=False)

time: 125 us -> 120 us (0.960)
  local copies, waits for them, and re-layouts: 3.16 us -> 0 us
    pallas_call x1, Pallas kernels: 121 us -> 117 us  [run_stage(): pl.pallas_call(functools.partial(stage_kernel, pp_size, heads), out_shape...]
    unnamed x1 -> x0, local copies, waits for them, and re-layouts: 3.16 us -> none
    pallas_call x0 -> x1, Pallas kernels: none -> 2.42 us  [settle(): pl.pallas_call(copy_kernel, out_shape=jax.ShapeDtypeStruct(x.shape, x.dty...]
where the time goes in v5:
time: 120 us
  Pallas kernels  120 us (100%)
    pallas_call x1, Pallas kernels, run_stage(): pl.pallas_call(functools.partial(stage_kernel, pp_size, heads), out_shape...  117 us
    pallas_call x1, Pallas kernels, settle(): pl.pallas_call(copy_kernel, out_shape=jax.ShapeDtypeStruct(x.shape, x.dty...  2.42 us

profile of v5, /device:TPU:0, one launch (start us, length us, event | category | flops | bytes accessed | tf_op | source)
XLA Modules:
  0.0 119.8 jit_solution(8151429587062921960)
XLA Ops:
  0.0 117.2 %shard_map.100.src = bf16[4,128,2048]{2,1,0:T(8,128)(2,1)} custom-call(bf16[16,320,2048]{2,1,0:T(8,128)(2,1)} %bitcast.16, s32[8,512]{1,0:T(8,128)} %bitcast.22, s32[8,512]{1,0:T(8,128)} %bitcast.23, f32[8,512]{1,0:T(8,128)} %bitcast.24, bf16[512,2048]{1,0:T(8,128)(2,1)} %bitcast.21, f32[1,2048]{1,0:T(1,128)} %scale_in.1, bf16[32768,128]{1,0:T(8,128)(2,1)} %bitcast.17, ...), custom_call_target="tpu_custom_call" | custom-call | tf_op jit(solution)/shard_map/pallas_call | solution.py:414
  117.2 2.4 %shard_map.101 = bf16[4,128,2048]{2,1,0:T(8,128)(2,1)} custom-call(bf16[4,128,2048]{2,1,0:T(8,128)(2,1)} %shard_map.100.src), custom_call_target="tpu_custom_call" | custom-call | tf_op jit(solution)/shard_map/pallas_call | solution.py:400

commit v6 on v5

--- a/solution.py
+++ b/solution.py
@@ -13,13 +13,12 @@
 COL = 512
 WIDE = 1024
 BLK = 128
-GROUP = 16
-PARTS = 4
+PARTS = 8
 
 
 def stage_kernel(pp_size, heads, o_hbm, ids_in, slot_in, gate_in, h_hbm, scale_in, wq_hbm, wk_hbm, wv_hbm, wo_hbm, out_hbm,
-                 arena, mine, theirs, tblt, gate_a, gate_b, ysend, acc, yrecv, dsend, drecv, hz, zrecv, panel, qbuf, kbuf, vbuf, xbuf,
-                 o_sem, h_sem, t_ssem, t_rsem, d_ssem, d_rsem, credit, y_ssem, y_rsem, z_ssem, z_rsem, yp_ssem, yp_rsem, zp_ssem, zp_rsem, s_sem, out_sem):
+                 arena, mine, theirs, tblt, gate_a, gate_b, ysend, acc, yrecv, dsend, drecv, hz, zrecv, panel, qbuf, kbuf, vbuf, xbuf, abuf,
+                 o_sem, h_sem, t_ssem, t_rsem, d_ssem, d_rsem, credit, y_ssem, y_rsem, z_ssem, z_rsem, yp_rsem, s_sem, out_sem):
     experts, cap_all, width = o_hbm.shape
     cap = cap_all // 4
     slots = experts * cap
@@ -52,37 +51,44 @@
 
     def h_copy(i):
         c, d = i // n_col, i % n_col
-        return pltpu.make_async_copy(h_hbm.at[pl.ds(c * TOK, TOK), pl.ds(d * COL, COL)], hz.at[i], h_sem.at[i])
-
-    def t_copy(r):
-        return pltpu.make_async_remote_copy(src_ref=mine, dst_ref=theirs.at[r], send_sem=t_ssem.at[r], recv_sem=t_rsem.at[r],
-                                            device_id={'ep': owners[r]}, device_id_type=MESH)
+        return pltpu.make_async_copy(h_hbm.at[pl.ds(c * TOK, TOK), pl.ds(d * COL, COL)], hz.at[i], h_sem.at[c])
+
+    cuts = (pl.ds(0, TOK), pl.ds(TOK, tokens - TOK))
+
+    def t_copy(r, part):
+        at = cuts[part]
+        return pltpu.make_async_remote_copy(src_ref=mine.at[:, at], dst_ref=theirs.at[r, :, at], send_sem=t_ssem.at[part, r],
+                                            recv_sem=t_rsem.at[part, r], device_id={'ep': owners[r]}, device_id_type=MESH)
 
     def d_copy(d):
         return pltpu.make_async_remote_copy(src_ref=dsend.at[d], dst_ref=drecv.at[d], send_sem=d_ssem.at[d],
                                             recv_sem=d_rsem.at[d], device_id={'ep': partner}, device_id_type=MESH)
 
     def y_copy(i):
-        return pltpu.make_async_remote_copy(src_ref=ysend.at[i], dst_ref=yrecv.at[i], send_sem=y_ssem.at[i], recv_sem=y_rsem.at[i],
+        return pltpu.make_async_remote_copy(src_ref=ysend.at[i], dst_ref=yrecv.at[i], send_sem=y_ssem, recv_sem=y_rsem.at[i],
                                             device_id={'ep': peer}, device_id_type=MESH)
 
     def z_copy(i):
         c, d = i // n_col, i % n_col
         return pltpu.make_async_remote_copy(src_ref=hz.at[i], dst_ref=zrecv.at[c, :, pl.ds(pl.multiple_of(d * COL, COL), COL)],
-                                            send_sem=z_ssem.at[i], recv_sem=z_rsem.at[i], device_id={'pp': nxt}, device_id_type=MESH)
-
+                                            send_sem=z_ssem, recv_sem=z_rsem.at[c], device_id={'pp': nxt}, device_id_type=MESH)
+
+    y_all = pltpu.make_async_remote_copy(src_ref=ysend, dst_ref=ysend, send_sem=y_ssem, recv_sem=y_rsem.at[0],
+                                         device_id={'ep': peer}, device_id_type=MESH)
+    z_all = pltpu.make_async_remote_copy(src_ref=hz, dst_ref=hz, send_sem=z_ssem, recv_sem=z_rsem.at[0],
+                                         device_id={'pp': nxt}, device_id_type=MESH)
     last = n_piece - 1
     thin = TOK // PARTS
 
     def y_part(k):
         rows = pl.ds(k * thin, thin)
-        return pltpu.make_async_remote_copy(src_ref=ysend.at[last, rows], dst_ref=yrecv.at[last, rows], send_sem=yp_ssem.at[k],
+        return pltpu.make_async_remote_copy(src_ref=ysend.at[last, rows], dst_ref=yrecv.at[last, rows], send_sem=y_ssem,
                                             recv_sem=yp_rsem.at[k], device_id={'ep': peer}, device_id_type=MESH)
 
     def z_part(k):
         rows = pl.ds(k * thin, thin)
         return pltpu.make_async_remote_copy(src_ref=hz.at[last, rows], dst_ref=zrecv.at[n_tok - 1, rows, pl.ds(width - COL, COL)],
-                                            send_sem=zp_ssem.at[k], recv_sem=zp_rsem.at[k], device_id={'pp': nxt}, device_id_type=MESH)
+                                            send_sem=z_ssem, recv_sem=z_rsem.at[n_tok - 1], device_id={'pp': nxt}, device_id_type=MESH)
 
     raw = (wq_hbm, wk_hbm, wv_hbm)
 
@@ -95,11 +101,10 @@
     def w_copy(q):
         return pltpu.make_async_copy(wo_hbm.at[:, pl.ds(q * head_dim, head_dim)], panel.at[q], s_sem.at[q])
 
-    lane_row = lax.broadcasted_iota(jnp.int32, (16, tokens), 0)
-
-    def keyed(r, table):
+    def keyed(r, table, part):
+        lane_row = lax.broadcasted_iota(jnp.int32, table.shape, 0)
         shift = jnp.where(lane_row < 8, me * slots, 0).astype(jnp.float32)
-        tblt[:, r * 16:(r + 1) * 16] = jnp.transpose(table - shift)
+        tblt[cuts[part], r * 16:(r + 1) * 16] = jnp.transpose(table - shift)
 
     groups = TOK // 16
 
@@ -150,7 +155,6 @@
             hz[last, rows] = (acc[last, rows] + yrecv[last, rows]).astype(jnp.bfloat16)
             z_part(k).start()
 
-    o_start(0)
     barrier = pltpu.get_barrier_semaphore()
     for dev in (partner, peer, diag):
         pl.semaphore_signal(barrier, inc=1, device_id={'ep': dev}, device_id_type=MESH)
@@ -159,25 +163,34 @@
     slot = slot_in[...]
     mine[0:8] = jnp.where(slot >= 0, ids_in[...] * cap + (slot - me * cap), -1).astype(jnp.float32)
     mine[8:16] = gate_in[...]
+    o_start(0)
     pl.semaphore_wait(barrier, 5)
-    for r in range(3):
-        t_copy(r).start()
+    for part in range(2):
+        for r in range(3):
+            t_copy(r, part).start()
     o_start(1)
-    keyed(3, mine[...])
-    for i in range(n_col):
-        h_copy(i).start()
-    for r in range(3):
-        t_copy(r).wait_recv()
-        keyed(r, theirs[r])
-        if r == 0:
-            build_now(0, 0)
-    o_start(2)
-    o_start(3)
-
-    def rest_h(i, _):
-        h_copy(i).start()
-        return 0
-    lax.fori_loop(n_col, n_piece, rest_h, 0)
+    for part in range(2):
+        keyed(3, mine[:, cuts[part]], part)
+
+    def table(r, part):
+        t_copy(r, part).wait_recv()
+        keyed(r, theirs[r, :, cuts[part]], part)
+
+    table(0, 0)
+    build_now(0, 0)
+    table(1, 0)
+
+    def later():
+        o_start(2)
+        o_start(3)
+
+        def one(i, _):
+            h_copy(i).start()
+            return 0
+        lax.fori_loop(0, n_piece, one, 0)
+        table(2, 0)
+        for r in range(3):
+            table(r, 1)
 
     def at_first(c, r):
         @pl.when(c == 0)
@@ -235,9 +248,9 @@
                 fill(d)
 
         def own_role(h, per, ahead=None):
-            for d in range(h, h + per):
-                h_copy(c * n_col + d).wait()
             if h == 0:
+                view = hz.at[pl.ds(c * n_col, n_col)]
+                pltpu.make_async_copy(view, view, h_sem.at[c]).wait()
                 at_first(c, 3)
             for d, value in dot_role(3, h, per):
                 i = c * n_col + d
@@ -254,10 +267,13 @@
 
         half = n_col // 2
         out_role(0, 0, 1, (c, 1))
+
         for d in range(1, half):
             out_role(0, d, 1)
         for d in range(half):
             near_role(d, 1)
+            if d == 0:
+                pl.when(c == 0)(later)
         out_role(0, half, half)
         near_role(half, half, (c, 2))
         out_role(2, 0, half, (c, 3))
@@ -289,16 +305,11 @@
 
     def out_copy(c, k):
         cols = pl.ds(k * WIDE, WIDE)
-        return pltpu.make_async_copy(zrecv.at[c, :, cols], out_hbm.at[c, :, cols], out_sem.at[c, k])
+        return pltpu.make_async_copy(zrecv.at[c, :, cols], out_hbm.at[c, :, cols], out_sem)
 
     def attend(c, hook):
         with jax.named_scope('zwait'):
-            for d in range(n_col):
-                if c * n_col + d < last:
-                    z_copy(c * n_col + d).wait_recv()
-                else:
-                    for k in range(PARTS):
-                        z_part(k).wait_recv()
+            pltpu.make_async_copy(zrecv.at[c], zrecv.at[c], z_rsem.at[c]).wait()
         scale = scale_in[...]
         for k in range(TOK // 16):
             rows = slice(k * 16, (k + 1) * 16)
@@ -306,35 +317,43 @@
             inv = lax.rsqrt(jnp.mean(x * x, axis=-1, keepdims=True) + NORM_EPS)
             xbuf[rows, :] = (x * inv * scale).astype(jnp.bfloat16)
 
-        def project(n, _):
-            cols = pl.ds(pl.multiple_of(n * WIDE, WIDE), WIDE)
+        seen = (c + 1) * TOK
+        q_at = lax.broadcasted_iota(jnp.int32, (TOK, seen), 0) + c * TOK
+        k_at = lax.broadcasted_iota(jnp.int32, (TOK, seen), 1)
+        causal = q_at >= k_at
+
+        def project(n, wide):
+            cols = pl.ds(n, wide)
             x = xbuf[...]
             qbuf[:, cols] = jnp.dot(x, arena[0:width, cols], preferred_element_type=jnp.float32).astype(jnp.bfloat16)
             kbuf[c * TOK:(c + 1) * TOK, cols] = jnp.dot(x, arena[width:2 * width, cols], preferred_element_type=jnp.float32).astype(jnp.bfloat16)
             vbuf[c * TOK:(c + 1) * TOK, cols] = jnp.dot(x, arena[2 * width:3 * width, cols], preferred_element_type=jnp.float32).astype(jnp.bfloat16)
-            return 0
-        with jax.named_scope('project'):
-            lax.fori_loop(0, halves, project, 0)
-        hook(0)
-        seen = (c + 1) * TOK
-        q_at = lax.broadcasted_iota(jnp.int32, (TOK, seen), 0) + c * TOK
-        k_at = lax.broadcasted_iota(jnp.int32, (TOK, seen), 1)
-        causal = q_at >= k_at
-
-        def head(h, _):
-            cols = [pl.ds(pl.multiple_of((h * GROUP + u) * head_dim, head_dim), head_dim) for u in range(GROUP)]
+
+        def mix(first, count):
+            cols = [pl.ds((first + u) * head_dim, head_dim) for u in range(count)]
             logits = [lax.dot_general(qbuf[:, at], kbuf[0:seen, at], (((1,), (1,)), ((), ())), preferred_element_type=jnp.float32) for at in cols]
             logits = [jnp.where(causal, s * (head_dim ** -0.5), -1e30) for s in logits]
             probs = [jnp.exp(s - jnp.max(s, axis=-1, keepdims=True)) for s in logits]
             sums = [jnp.sum(p, axis=-1, keepdims=True) for p in probs]
             mixed = [jnp.dot(p.astype(jnp.bfloat16), vbuf[0:seen, at], preferred_element_type=jnp.float32) for p, at in zip(probs, cols)]
             for at, m, t in zip(cols, mixed, sums):
-                xbuf[:, at] = (m / t).astype(jnp.bfloat16)
-            return 0
-        with jax.named_scope('heads'):
-            lax.fori_loop(0, heads // GROUP, head, 0)
-        hook(1)
-
+                abuf[:, at] = (m / t).astype(jnp.bfloat16)
+
+        if c == n_tok - 1:
+            with jax.named_scope('lastmix'):
+                for k in range(halves):
+                    project(k * WIDE, WIDE)
+                    mix(k * heads // halves, heads // halves)
+        else:
+            def one(n, _):
+                project(pl.multiple_of(n * WIDE, WIDE), WIDE)
+                return 0
+            with jax.named_scope('project'):
+                lax.fori_loop(0, halves, one, 0)
+            hook(0)
+            with jax.named_scope('heads'):
+                mix(0, heads)
+            hook(1)
         if c == 0:
             for q in range(heads):
                 w_copy(q).wait()
@@ -342,7 +361,7 @@
             for k in range(halves):
                 cols = slice(k * WIDE, (k + 1) * WIDE)
                 w = jnp.concatenate([panel[q] for q in range(k * WIDE // head_dim, (k + 1) * WIDE // head_dim)], axis=1)
-                proj = jnp.dot(xbuf[...], w, preferred_element_type=jnp.float32).astype(jnp.bfloat16)
+                proj = jnp.dot(abuf[...], w, preferred_element_type=jnp.float32).astype(jnp.bfloat16)
                 zrecv[c, :, cols] = (zrecv[c, :, cols].astype(jnp.float32) + proj.astype(jnp.float32)).astype(jnp.bfloat16)
                 out_copy(c, k).start()
         hook(2)
@@ -366,21 +385,14 @@
         with jax.named_scope('attend'):
             attend(c, hook)
 
-    def drain(i, _):
-        y_copy(i).wait_send()
-        z_copy(i).wait_send()
-        return 0
-    lax.fori_loop(0, last, drain, 0)
-    for k in range(PARTS):
-        y_part(k).wait_send()
-        z_part(k).wait_send()
+    y_all.wait_send()
+    z_all.wait_send()
     for d in range(n_col):
         d_copy(d).wait_send()
-    for r in range(3):
-        t_copy(r).wait_send()
-    for c in range(n_tok):
-        for k in range(halves):
-            out_copy(c, k).wait()
+    for part in range(2):
+        for r in range(3):
+            t_copy(r, part).wait_send()
+    pltpu.make_async_copy(zrecv, out_hbm, out_sem).wait()
 
 
 def copy_kernel(src, dst, hold, in_sem, out_sem):
@@ -426,10 +438,10 @@
             pltpu.VMEM((n_piece, TOK, COL), bf16),
             pltpu.VMEM((n_tok, TOK, width), bf16),
             pltpu.VMEM((width // BLK, width, width // heads), bf16),
-            pltpu.VMEM((TOK, width), bf16), pltpu.VMEM((tokens, width), bf16), pltpu.VMEM((tokens, width), bf16), pltpu.VMEM((TOK, width), bf16),
-            dma((4,)), dma((n_piece,)), dma((3,)), dma((3,)), dma((n_col,)), dma((n_col,)),
+            pltpu.VMEM((TOK, width), bf16), pltpu.VMEM((tokens, width), bf16), pltpu.VMEM((tokens, width), bf16), pltpu.VMEM((TOK, width), bf16), pltpu.VMEM((TOK, width), bf16),
+            dma((4,)), dma((n_tok,)), dma((2, 3)), dma((2, 3)), dma((n_col,)), dma((n_col,)),
             pltpu.SemaphoreType.REGULAR,
-            dma((n_piece,)), dma((n_piece,)), dma((n_piece,)), dma((n_piece,)), dma((PARTS,)), dma((PARTS,)), dma((PARTS,)), dma((PARTS,)), dma((width // BLK,)), dma((n_tok, width // WIDE)),
+            dma, dma((n_piece - 1,)), dma, dma((n_tok,)), dma((PARTS,)), dma((width // BLK,)), dma,
         ],
         compiler_params=pltpu.CompilerParams(collective_id=0, has_side_effects=True, vmem_limit_bytes=67043328),
     )(expert_out, ids, slot, gate, resid, scale, wq, wk, wv, wo)

time: 120 us -> 117 us (0.975)
  Pallas kernels: 120 us -> 117 us
    pallas_call x1, Pallas kernels: 117 us -> 115 us  [run_stage(): pl.pallas_call(functools.partial(stage_kernel, pp_size, heads), out_shape...]
where the time goes in v6:
time: 117 us
  Pallas kernels  117 us (100%)
    pallas_call x1, Pallas kernels, run_stage(): pl.pallas_call(functools.partial(stage_kernel, pp_size, heads), out_shape...  115 us
    pallas_call x1, Pallas kernels, settle(): pl.pallas_call(copy_kernel, out_shape=jax.ShapeDtypeStruct(x.shape, x.dty...  2.42 us

profile of v6, /device:TPU:0, one launch (start us, length us, event | category | flops | bytes accessed | tf_op | source)
XLA Modules:
  0.0 117.2 jit_solution(6572261955105091458)
XLA Ops:
  0.0 114.6 %shard_map.100.src = bf16[4,128,2048]{2,1,0:T(8,128)(2,1)} custom-call(bf16[16,320,2048]{2,1,0:T(8,128)(2,1)} %bitcast.16, s32[8,512]{1,0:T(8,128)} %bitcast.22, s32[8,512]{1,0:T(8,128)} %bitcast.23, f32[8,512]{1,0:T(8,128)} %bitcast.24, bf16[512,2048]{1,0:T(8,128)(2,1)} %bitcast.21, f32[1,2048]{1,0:T(1,128)} %scale_in.1, bf16[32768,128]{1,0:T(8,128)(2,1)} %bitcast.17, ...), custom_call_target="tpu_custom_call" | custom-call | tf_op jit(solution)/shard_map/pallas_call | solution.py:426
  114.6 2.4 %shard_map.101 = bf16[4,128,2048]{2,1,0:T(8,128)(2,1)} custom-call(bf16[4,128,2048]{2,1,0:T(8,128)(2,1)} %shard_map.100.src), custom_call_target="tpu_custom_call" | custom-call | tf_op jit(solution)/shard_map/pallas_call | solution.py:412

commit v7 on v6

--- a/solution.py
+++ b/solution.py
@@ -16,8 +16,8 @@
 PARTS = 8
 
 
-def stage_kernel(pp_size, heads, o_hbm, ids_in, slot_in, gate_in, h_hbm, scale_in, wq_hbm, wk_hbm, wv_hbm, wo_hbm, out_hbm,
-                 arena, mine, theirs, tblt, gate_a, gate_b, ysend, acc, yrecv, dsend, drecv, hz, zrecv, panel, qbuf, kbuf, vbuf, xbuf, abuf,
+def stage_kernel(pp_size, heads, o_hbm, ids_hbm, slot_hbm, gate_hbm, h_hbm, scale_hbm, wq_hbm, wk_hbm, wv_hbm, wo_hbm, out_hbm,
+                 ids_in, slot_in, gate_in, scale_in, i_sem, arena, mine, theirs, tblt, gate_a, gate_b, ysend, acc, yrecv, dsend, drecv, hz, zrecv, panel, qbuf, kbuf, vbuf, xbuf, abuf,
                  o_sem, h_sem, t_ssem, t_rsem, d_ssem, d_rsem, credit, y_ssem, y_rsem, z_ssem, z_rsem, yp_rsem, s_sem, out_sem):
     experts, cap_all, width = o_hbm.shape
     cap = cap_all // 4
@@ -155,15 +155,25 @@
             hz[last, rows] = (acc[last, rows] + yrecv[last, rows]).astype(jnp.bfloat16)
             z_part(k).start()
 
+    smalls = ((ids_hbm, ids_in), (slot_hbm, slot_in), (gate_hbm, gate_in), (scale_hbm, scale_in))
+
+    def small(k):
+        return pltpu.make_async_copy(*smalls[k], i_sem.at[k])
+
     barrier = pltpu.get_barrier_semaphore()
     for dev in (partner, peer, diag):
         pl.semaphore_signal(barrier, inc=1, device_id={'ep': dev}, device_id_type=MESH)
     for dev in (nxt, prv):
         pl.semaphore_signal(barrier, inc=1, device_id={'pp': dev}, device_id_type=MESH)
+    for k in range(3):
+        small(k).start()
+    o_start(0)
+    small(3).start()
+    for k in range(3):
+        small(k).wait()
     slot = slot_in[...]
     mine[0:8] = jnp.where(slot >= 0, ids_in[...] * cap + (slot - me * cap), -1).astype(jnp.float32)
     mine[8:16] = gate_in[...]
-    o_start(0)
     pl.semaphore_wait(barrier, 5)
     for part in range(2):
         for r in range(3):
@@ -183,6 +193,7 @@
     def later():
         o_start(2)
         o_start(3)
+        small(3).wait()
 
         def one(i, _):
             h_copy(i).start()
@@ -421,14 +432,14 @@
     n_piece = n_tok * n_col
     dma = pltpu.SemaphoreType.DMA
     anyspace = pl.BlockSpec(memory_space=pl.ANY)
-    vmem = pl.BlockSpec(memory_space=pltpu.VMEM)
     f32, bf16 = jnp.float32, jnp.bfloat16
     return pl.pallas_call(
         functools.partial(stage_kernel, pp_size, heads),
         out_shape=jax.ShapeDtypeStruct((n_tok, TOK, width), bf16),
-        in_specs=[anyspace, vmem, vmem, vmem, anyspace, vmem, anyspace, anyspace, anyspace, anyspace],
+        in_specs=[anyspace] * 10,
         out_specs=anyspace,
         scratch_shapes=[
+            pltpu.VMEM(ids.shape, jnp.int32), pltpu.VMEM(slot.shape, jnp.int32), pltpu.VMEM(gate.shape, f32), pltpu.VMEM(scale.shape, f32), dma((4,)),
             pltpu.VMEM((max(4 * slots, 3 * width), width), bf16),
             pltpu.VMEM((16, tokens), f32), pltpu.VMEM((3, 16, tokens), f32),
             pltpu.VMEM((tokens, 64), f32),

time: 117 us -> 117 us (level)
  no operation moved by 1% of the time
where the time goes in v7:
time: 117 us; the launch traced here: 116 us
  Pallas kernels  116 us (99%)
    pallas_call x1, Pallas kernels, run_stage(): pl.pallas_call(functools.partial(stage_kernel, pp_size, heads), out_shape...  114 us
    pallas_call x1, Pallas kernels, settle(): pl.pallas_call(copy_kernel, out_shape=jax.ShapeDtypeStruct(x.shape, x.dty...  2.42 us

profile of v7, /device:TPU:0, one launch (start us, length us, event | category | flops | bytes accessed | tf_op | source)
XLA Modules:
  0.0 116.5 jit_solution(5342901327933102672)
XLA Ops:
  0.0 113.9 %shard_map.100.src = bf16[4,128,2048]{2,1,0:T(8,128)(2,1)} custom-call(bf16[16,320,2048]{2,1,0:T(8,128)(2,1)} %bitcast.16, s32[8,512]{1,0:T(8,128)} %bitcast.22, s32[8,512]{1,0:T(8,128)} %bitcast.23, f32[8,512]{1,0:T(8,128)} %bitcast.24, bf16[512,2048]{1,0:T(8,128)(2,1)} %bitcast.21, f32[1,2048]{1,0:T(1,128)} %scale_hbm.1, bf16[32768,128]{1,0:T(8,128)(2,1)} %bitcast.17, ...), custom_call_target="tpu_custom_call" | custom-call | tf_op jit(solution)/shard_map/pallas_call | solution.py:436
  113.9 2.4 %shard_map.101 = bf16[4,128,2048]{2,1,0:T(8,128)(2,1)} custom-call(bf16[4,128,2048]{2,1,0:T(8,128)(2,1)} %shard_map.100.src), custom_call_target="tpu_custom_call" | custom-call | tf_op jit(solution)/shard_map/pallas_call | solution.py:423
